TPU v7x, 16 devices: a whole 2x2x2 slice. The times are simulated.
16 devices in a mesh: dp: 4 (over z, y), tp: 4 (over x, core).
Axes of the slice: x: 2, y: 2, z: 2, core: 2. Of those that a mesh axis runs over, the one named last changes fastest.
Arguments:
- patches: bfloat16 [96, 256, 768], P('dp', 'tp'), parts along dimension 0
- patch_w: bfloat16 [768, 1024], replicated
- patch_b: bfloat16 [1024], replicated
- pos_emb: bfloat16 [256, 1024], P('tp')
- ln_scale: bfloat16 [2, 1024], replicated
- ln_bias: bfloat16 [2, 1024], replicated
- qkv_w: bfloat16 [3, 1024, 16, 64], P(None, None, 'tp')
- qkv_b: bfloat16 [3, 16, 64], P(None, 'tp')
- out_w: bfloat16 [16, 64, 1024], P('tp')
- out_b: bfloat16 [1024], replicated
- fc1_w: bfloat16 [1024, 4096], P(None, 'tp')
- fc1_b: bfloat16 [4096], P('tp')
- fc2_w: bfloat16 [4096, 1024], P('tp')
- fc2_b: bfloat16 [1024], replicated
- d_out: bfloat16 [96, 256, 1024], P('dp', 'tp'), parts along dimension 0
Outputs:
- output 1: bfloat16 [96, 256, 1024], P('dp', 'tp'), parts along dimension 0
- output 2: bfloat16 [3072, 1024], P('dp'), parts along dimension 0
- output 3: bfloat16 [4096], P('dp'), parts along dimension 0
- output 4: bfloat16 [1024, 1024], P(('dp', 'tp')), parts along dimension 0
- output 5: bfloat16 [8, 1024], P('dp'), parts along dimension 0
- output 6: bfloat16 [8, 1024], P('dp'), parts along dimension 0
- output 7: bfloat16 [12, 1024, 16, 64], P('dp', None, 'tp'), parts along dimension 0
- output 8: bfloat16 [12, 16, 64], P('dp', 'tp'), parts along dimension 0
- output 9: bfloat16 [64, 64, 1024], P(('dp', 'tp')), parts along dimension 0
- output 10: bfloat16 [4096], P('dp'), parts along dimension 0
- output 11: bfloat16 [4096, 4096], P('dp', 'tp'), parts along dimension 0
- output 12: bfloat16 [16384], P(('dp', 'tp')), parts along dimension 0
- output 13: bfloat16 [16384, 1024], P(('dp', 'tp')), parts along dimension 0
- output 14: bfloat16 [4096], P('dp'), parts along dimension 0
There are 4 independent parts. A program takes and returns all parts, laid end to end along the dimension named above; an argument that names none is the same for every part.
All inputs are finite; a program needn't handle non-finite values.
Results may differ from a plain program's by a relative error of at most 0.02.
Values are sent between devices in bfloat16 or wider.
A program may use at most 1 GiB of HBM per device.

v0:
```python
import jax
import jax.numpy as jnp
from jax import lax
from jax.sharding import PartitionSpec as P

LN_EPS = 1e-6


def layer_norm(x_val, scale_f, bias_f):
    row_mean = jnp.mean(x_val, axis=-1, keepdims=True)
    centered = x_val - row_mean
    row_var = jnp.mean(centered * centered, axis=-1, keepdims=True)
    return centered * lax.rsqrt(row_var + LN_EPS) * scale_f + bias_f


def gelu_tanh(pre_act):
    return jax.nn.gelu(pre_act, approximate=True)


def group_step(patches, patch_w, patch_b, pos_emb, ln_scale, ln_bias, qkv_w, qkv_b, out_w, out_b, fc1_w, fc1_b, fc2_w, fc2_b, d_out):
    wide = jnp.float32
    half = jnp.bfloat16
    scale = qkv_w.shape[-1] ** -0.5
    ln_scale_f = ln_scale.astype(wide)
    ln_bias_f = ln_bias.astype(wide)
    emb = jnp.einsum('btp,pd->btd', patches, patch_w, preferred_element_type=wide)
    emb_f = (emb + patch_b.astype(wide) + pos_emb.astype(wide)).astype(half).astype(wide)
    h_one_f, ln_one_vjp = jax.vjp(layer_norm, emb_f, ln_scale_f[0], ln_bias_f[0])
    h_one_all = lax.all_gather(h_one_f.astype(half), 'tp', axis=1, tiled=True)
    qkv = jnp.einsum('btd,sdhc->btshc', h_one_all, qkv_w, preferred_element_type=wide)
    qkv = (qkv + qkv_b.astype(wide)).astype(half)
    query = qkv[:, :, 0]
    keys_all = qkv[:, :, 1]
    values = qkv[:, :, 2]
    scores = jnp.einsum('bqhc,bkhc->bhqk', query, keys_all, preferred_element_type=wide) * scale
    probs = jax.nn.softmax(scores, axis=-1)
    probs_h = probs.astype(half)
    context = jnp.einsum('bhqk,bkhc->bqhc', probs_h, values, preferred_element_type=wide).astype(half)
    attn_part = jnp.einsum('crid,ide->cre', context, out_w, preferred_element_type=wide)
    attn_out = lax.psum_scatter(attn_part, 'tp', scatter_dimension=1, tiled=True)
    x_one_f = (emb_f + (attn_out + out_b.astype(wide))).astype(half).astype(wide)
    h_two_f, ln_two_vjp = jax.vjp(layer_norm, x_one_f, ln_scale_f[1], ln_bias_f[1])
    h_two_all = lax.all_gather(h_two_f.astype(half), 'tp', axis=1, tiled=True)
    pre_act = jnp.einsum('btd,df->btf', h_two_all, fc1_w, preferred_element_type=wide) + fc1_b.astype(wide)
    hidden_f, gelu_vjp = jax.vjp(gelu_tanh, pre_act)
    hidden = hidden_f.astype(half)
    mlp_part = jnp.einsum('btf,fd->btd', hidden, fc2_w, preferred_element_type=wide)
    mlp_out = lax.psum_scatter(mlp_part, 'tp', scatter_dimension=1, tiled=True)
    x_two = (x_one_f + (mlp_out + fc2_b.astype(wide))).astype(half)
    d_two_f = d_out.astype(wide)
    d_fc2_b = jnp.sum(d_two_f, axis=(0, 1))
    d_out_all = lax.all_gather(d_out, 'tp', axis=1, tiled=True)
    d_fc2_w = jnp.einsum('btf,btd->fd', hidden, d_out_all, preferred_element_type=wide)
    d_hidden = jnp.einsum('btd,fd->btf', d_out_all, fc2_w, preferred_element_type=wide).astype(half)
    d_pre = gelu_vjp(d_hidden.astype(wide))[0]
    d_fc1_b = jnp.sum(d_pre, axis=(0, 1))
    d_pre_h = d_pre.astype(half)
    d_fc1_w = jnp.einsum('btd,btf->df', h_two_all, d_pre_h, preferred_element_type=wide)
    d_h_two_part = jnp.einsum('btf,df->btd', d_pre_h, fc1_w, preferred_element_type=wide)
    d_h_two = lax.psum_scatter(d_h_two_part, 'tp', scatter_dimension=1, tiled=True).astype(half)
    d_x_ln, d_ln2_scale, d_ln2_bias = ln_two_vjp(d_h_two.astype(wide))
    d_x_one = (d_two_f + d_x_ln).astype(half)
    d_out_b = jnp.sum(d_x_one, axis=(0, 1), dtype=wide)
    d_x_one_all = lax.all_gather(d_x_one, 'tp', axis=1, tiled=True)
    d_out_w = jnp.einsum('crid,cre->ide', context, d_x_one_all, preferred_element_type=wide)
    d_context = jnp.einsum('cre,ide->crid', d_x_one_all, out_w, preferred_element_type=wide).astype(half)
    d_values = jnp.einsum('bhqk,bqhc->bkhc', probs_h, d_context, preferred_element_type=wide).astype(half)
    d_probs = jnp.einsum('bqhc,bkhc->bhqk', d_context, values, preferred_element_type=wide).astype(half).astype(wide)
    d_scores = probs * (d_probs - jnp.sum(d_probs * probs, axis=-1, keepdims=True))
    d_scores_h = (d_scores * scale).astype(half)
    d_query = jnp.einsum('bhqk,bkhc->bqhc', d_scores_h, keys_all, preferred_element_type=wide).astype(half)
    d_keys = jnp.einsum('bhqk,bqhc->bkhc', d_scores_h, query, preferred_element_type=wide).astype(half)
    d_qkv = jnp.stack([d_query, d_keys, d_values], axis=2)
    d_qkv_b = jnp.sum(d_qkv, axis=(0, 1), dtype=wide)
    d_qkv_w = jnp.einsum('btd,btshc->sdhc', h_one_all, d_qkv, preferred_element_type=wide)
    d_h_one_part = jnp.einsum('btshc,sdhc->btd', d_qkv, qkv_w, preferred_element_type=wide)
    d_h_one = lax.psum_scatter(d_h_one_part, 'tp', scatter_dimension=1, tiled=True).astype(half)
    d_emb_ln, d_ln1_scale, d_ln1_bias = ln_one_vjp(d_h_one.astype(wide))
    d_emb = (d_x_one.astype(wide) + d_emb_ln).astype(half)
    d_pos = jnp.sum(d_emb, axis=0, dtype=wide)
    d_patch_b = jnp.sum(d_emb, axis=(0, 1), dtype=wide)
    d_patch_w = jnp.einsum('btp,btd->pd', patches, d_emb, preferred_element_type=wide)
    d_ln_scale = jnp.stack([d_ln1_scale, d_ln2_scale])
    d_ln_bias = jnp.stack([d_ln1_bias, d_ln2_bias])
    d_patch_w, d_patch_b, d_ln_scale, d_ln_bias, d_out_b, d_fc2_b = lax.psum((d_patch_w, d_patch_b, d_ln_scale, d_ln_bias, d_out_b, d_fc2_b), 'tp')
    return (x_two, d_patch_w.astype(half), d_patch_b.astype(half), d_pos.astype(half), d_ln_scale.astype(half), d_ln_bias.astype(half), d_qkv_w.astype(half), d_qkv_b.astype(half), d_out_w.astype(half), d_out_b.astype(half), d_fc1_w.astype(half), d_fc1_b.astype(half), d_fc2_w.astype(half), d_fc2_b.astype(half))


def solution(mesh):
    in_specs = (P('dp', 'tp', None), P(), P(), P('tp', None), P(), P(), P(None, None, 'tp', None), P(None, 'tp', None), P('tp', None, None), P(), P(None, 'tp'), P('tp'), P('tp', None), P(), P('dp', 'tp', None))
    out_specs = (P('dp', 'tp', None), P('dp', None), P('dp'), P(('dp', 'tp'), None), P('dp', None), P('dp', None), P('dp', None, 'tp', None), P('dp', 'tp', None), P(('dp', 'tp'), None, None), P('dp'), P('dp', 'tp'), P(('dp', 'tp')), P(('dp', 'tp'), None), P('dp'))
    return jax.shard_map(group_step, mesh=mesh, in_specs=in_specs, out_specs=out_specs, check_vma=False)
```

profile of v0, /device:TPU:0, one launch (start us, length us, event | category | flops | bytes accessed | tf_op | source)
XLA Modules:
  0.0 1373.6 jit_solution(14121878193720092670)
XLA Ops:
  7.2 0.0 all-gather.5.cloned.1.call-start
  7.2 0.8 convert_element_type.167
  8.1 0.8 fusion.120
  8.9 0.8 fusion.121
  9.6 0.9 convert_element_type.168
  10.6 4.4 convert_reduce_fusion.3
  15.0 1.0 fusion.49
  16.0 0.6 copy-done.18
  16.7 0.6 copy-done.14
  17.2 2.5 fusion.46
  19.7 0.2 reduce-scatter.5.cloned.1.call-start
  20.0 83.6 %all-gather.5.cloned.1.call-done = bf16[24,256,1024]{2,1,0:T(8,128)(2,1)} async-done(((bf16[24,64,1024]{2,1,0:T(8,128)(2,1)}), bf16[24,256,1024]{2,1,0:T(8,128)(2,1)}) %all-gather.5.cloned.1.call-update) | async-done | bytes 12582928 | tf_op jit(solution)/shard_map/all_gather | solution.py:29
  103.6 15.6 %add_convert_fusion = bf16[24,256,3,4,64]{1,4,3,2,0:T(8,128)(2,1)} fusion(f32[3,4,64]{2,1,0:T(4,128)S(1)} %convert_element_type.174, bf16[24,256,1024]{2,1,0:T(8,128)(2,1)} %all-gather.5.cloned.1.call-done, bf16[3,1024,4,64]{1,3,2,0:T(8,128)(2,1)} %param.21), kind=kOutput, calls=%fused_computation.24 | convolution fusion | flops 9673113600 | bytes 23596032 | tf_op jit(solution)/shard_map/btd,sdhc->btshc/dot_general | solution.py:30
  119.1 14.9 %fusion.122 = (f32[24,4,256]{2,1,0:T(4,128)S(1)}, f32[24,4,256,256]{2,3,1,0:T(8,128)}) fusion(bf16[24,256,3,4,64]{1,4,3,2,0:T(8,128)(2,1)} %add_convert_fusion), kind=kOutput, calls=%fused_computation.149 | convolution fusion | flops 824180992 | bytes 31555584 | tf_op jit(solution)/shard_map/sub | solution.py:36
  134.1 13.2 fusion.72
  147.3 12.0 convolution_bitcast_fusion.1
  159.3 0.3 all-gather.7.cloned.1.call-start
  159.6 0.4 copy-done.33
  160.0 170.4 %reduce-scatter.5.cloned.1.call-done = f32[24,64,1024]{2,1,0:T(8,128)} async-done(((f32[24,256,1024]{2,1,0:T(8,128)}), f32[24,64,1024]{2,1,0:T(8,128)}) %reduce-scatter.5.cloned.1.call-update) | async-done | bytes 6291472 | tf_op jit(solution)/shard_map/reduce_scatter | solution.py:40
  330.4 4.7 convert_reduce_fusion.2
  335.1 1.0 fusion.52
  336.2 0.6 copy-done.20
  336.8 0.6 copy-done.16
  337.4 2.5 fusion.44
  339.9 0.0 all-gather.7.cloned.1.call-update
  339.9 0.0 all-gather.9.cloned.1.call-start
  340.0 0.5 all-gather.9.cloned.1.call-update
  340.5 0.0 reduce-scatter.9.cloned.1.call-start
  340.6 80.4 %all-gather.7.cloned.1.call-done = bf16[24,256,1024]{2,1,0:T(8,128)(2,1)} async-done(((bf16[24,64,1024]{2,1,0:T(8,128)(2,1)}), bf16[24,256,1024]{2,1,0:T(8,128)(2,1)}) %all-gather.7.cloned.1.call-update) | async-done | bytes 12582928 | tf_op jit(solution)/shard_map/all_gather | solution.py:43
  420.9 21.3 %fusion.86 = f32[24,256,1024]{2,1,0:T(8,128)} fusion(bf16[24,256,1024]{2,1,0:T(8,128)(2,1)} %all-gather.7.cloned.1.call-done, bf16[1024,1024]{1,0:T(8,128)(2,1)} %param.25), kind=kOutput, calls=%fused_computation.117 | convolution fusion | flops 12884901888 | bytes 39845888 | tf_op jit(solution)/shard_map/btd,df->btf/dot_general | solution.py:44
  442.2 61.0 %all-gather.9.cloned.1.call-done = bf16[24,256,1024]{2,1,0:T(8,128)(2,1)} async-done(((bf16[24,64,1024]{2,1,0:T(8,128)(2,1)}), bf16[24,256,1024]{2,1,0:T(8,128)(2,1)}) %all-gather.9.cloned.1.call-update) | async-done | bytes 12582928 | tf_op jit(solution)/shard_map/all_gather | solution.py:52
  503.2 38.2 %fusion.123 = (bf16[1024]{0:T(1024)(128)(2,1)}, bf16[24,256,1024]{2,1,0:T(8,128)(2,1)}) fusion(f32[24,256,1024]{2,1,0:T(8,128)} %fusion.86, f32[1024]{0:T(1024)S(1)} %convert_element_type.183, bf16[24,256,1024]{2,1,0:T(8,128)(2,1)} %all-gather.9.cloned.1.call-done, bf16[1024,1024]{1,0:T(8,128)(2,1)} %param.27), kind=kOutput, calls=%fused_computation.150 | convolution fusion | flops 13035895808 | bytes 52434944 | tf_op jit(solution)/shard_map/btd,fd->btf/dot_general | solution.py:54
  541.5 21.0 %fusion.59 = f32[24,256,1024]{2,1,0:T(8,128)} fusion(bf16[24,256,1024]{2,1,0:T(8,128)(2,1)} %get-tuple-element.61, bf16[1024,1024]{1,0:T(8,128)(2,1)S(1)} %copy-done.36), kind=kOutput, calls=%fused_computation.89 | convolution fusion | flops 12884901888 | bytes 39845888 | tf_op jit(solution)/shard_map/btf,df->btd/dot_general | solution.py:59
  562.5 0.0 reduce-scatter.7.cloned.1.call-start
  562.6 26.8 %fusion.83 = f32[24,256,1024]{2,1,0:T(8,128)} fusion(bf16[1024,1024]{1,0:T(8,128)(2,1)} %param.27, f32[24,256,1024]{2,1,0:T(8,128)} %fusion.86, f32[1024]{0:T(1024)S(1)} %convert_element_type.183), kind=kOutput, calls=%fused_computation.114 | convolution fusion | flops 12947816448 | bytes 52432896 | tf_op jit(solution)/shard_map/btf,fd->btd/dot_general | solution.py:47
  589.3 0.0 reduce-scatter.7.cloned.1.call-update
  589.4 0.0 all-gather.11.cloned.1.call-start
  589.4 0.6 copy-done.35
  590.0 143.6 %reduce-scatter.9.cloned.1.call-done = f32[24,64,1024]{2,1,0:T(8,128)} async-done(((f32[24,256,1024]{2,1,0:T(8,128)}), f32[24,64,1024]{2,1,0:T(8,128)}) %reduce-scatter.9.cloned.1.call-update) | async-done | bytes 6291472 | tf_op jit(solution)/shard_map/reduce_scatter | solution.py:60
  733.6 5.3 convert_reduce_fusion.1
  739.0 4.3 fusion.55
  743.3 163.7 %reduce-scatter.7.cloned.1.call-done = f32[24,64,1024]{2,1,0:T(8,128)} async-done(((f32[24,256,1024]{2,1,0:T(8,128)}), f32[24,64,1024]{2,1,0:T(8,128)}) %reduce-scatter.7.cloned.1.call-update) | async-done | bytes 6291472 | tf_op jit(solution)/shard_map/reduce_scatter | solution.py:48
  907.0 11.0 convert_reduce_fusion.4
  918.1 0.0 reduce-scatter.11.cloned.1.call-start
  918.1 81.0 %all-gather.11.cloned.1.call-done = bf16[24,256,1024]{2,1,0:T(8,128)(2,1)} async-done(((bf16[24,64,1024]{2,1,0:T(8,128)(2,1)}), bf16[24,256,1024]{2,1,0:T(8,128)(2,1)}) %all-gather.11.cloned.1.call-update) | async-done | bytes 12582928 | tf_op jit(solution)/shard_map/all_gather | solution.py:64
  999.1 14.7 %fusion.77 = bf16[24,256,4,64]{1,3,2,0:T(8,128)(2,1)} fusion(bf16[24,256,1024]{2,1,0:T(8,128)(2,1)} %all-gather.11.cloned.1.call-done, bf16[4,64,1024]{2,1,0:T(8,128)(2,1)S(1)} %copy-done.38), kind=kOutput, calls=%fused_computation.112 | convolution fusion | flops 3222798336 | bytes 16252928 | tf_op jit(solution)/shard_map/cre,ide->crid/dot_general | solution.py:66
  1013.8 13.2 convert_bitcast_fusion
  1027.1 10.8 convolution_convert_fusion
  1037.8 32.0 %convert_bitcast_fusion.2 = bf16[24,256,1,4,64]{1,4,3,0,2:T(8,128)(2,1)} fusion(bf16[24,4,256,256]{2,3,1,0:T(8,128)(2,1)} %convolution_convert_fusion, bf16[24,256,3,4,64]{1,4,3,2,0:T(8,128)(2,1)} %add_convert_fusion, f32[24,4,256,256]{2,3,1,0:T(8,128)} %get-tuple-element.59, f32[24,4,256]{2,1,0:T(4,128)S(1)} %copy-done.41), kind=kOutput, calls=%fused_computation.109 | convolution fusion | flops 863527168 | bytes 81985536 | tf_op jit(solution)/shard_map/bhqk,bkhc->bqhc/dot_general | solution.py:71
  1069.8 28.4 %convert_bitcast_fusion.1 = bf16[24,256,1,4,64]{1,4,3,0,2:T(8,128)(2,1)} fusion(bf16[24,4,256,256]{2,3,1,0:T(8,128)(2,1)} %convolution_convert_fusion, bf16[24,256,3,4,64]{1,4,3,2,0:T(8,128)(2,1)} %add_convert_fusion, f32[24,4,256,256]{2,3,1,0:T(8,128)} %get-tuple-element.59, f32[24,4,256]{2,1,0:T(4,128)S(1)} %copy-done.41), kind=kOutput, calls=%fused_computation.108 | convolution fusion | flops 863527168 | bytes 81985536 | tf_op jit(solution)/shard_map/bhqk,bqhc->bkhc/dot_general | solution.py:72
  1098.2 18.0 %convolution_bitcast_fusion = f32[24,256,1024]{2,1,0:T(8,128)} fusion(bf16[3,1024,4,64]{1,3,2,0:T(8,128)(2,1)} %param.21, bf16[24,256,1,4,64]{1,4,3,0,2:T(8,128)(2,1)} %convert_bitcast_fusion, bf16[24,256,1,4,64]{1,4,3,0,2:T(8,128)(2,1)} %convert_bitcast_fusion.1, bf16[24,256,1,4,64]{1,4,3,0,2:T(8,128)(2,1)} %convert_bitcast_fusion.2), kind=kOutput, calls=%fused_computation.61 | convolution fusion | flops 9673113600 | bytes 36175872 | tf_op jit(solution)/shard_map/btshc,sdhc->btd/dot_general | solution.py:76
  1116.2 19.1 %bitcast_convert_fusion.1 = bf16[1024,1024]{1,0:T(8,128)(2,1)} fusion(bf16[24,256,1024]{2,1,0:T(8,128)(2,1)} %all-gather.7.cloned.1.call-done, bf16[24,256,1024]{2,1,0:T(8,128)(2,1)} %get-tuple-element.61), kind=kOutput, calls=%fused_computation.97 | convolution fusion | flops 12885950464 | bytes 27262976 | tf_op jit(solution)/shard_map/btd,btf->df/dot_general | solution.py:58
  1135.3 23.0 %bitcast_convert_fusion = bf16[1024,1024]{1,0:T(8,128)(2,1)} fusion(bf16[24,256,1024]{2,1,0:T(8,128)(2,1)} %all-gather.9.cloned.1.call-done, f32[24,256,1024]{2,1,0:T(8,128)} %fusion.86, f32[1024]{0:T(1024)S(1)} %copy-done.31), kind=kOutput, calls=%fused_computation.96 | convolution fusion | flops 12948865024 | bytes 39849984 | tf_op jit(solution)/shard_map/btf,btd->fd/dot_general | solution.py:53
  1158.3 5.8 fusion.115
  1164.1 7.7 fusion.101
  1171.8 15.7 %fusion.93 = bf16[3,1024,4,64]{1,3,2,0:T(8,128)(2,1)} fusion(bf16[24,256,1024]{2,1,0:T(8,128)(2,1)} %all-gather.5.cloned.1.call-done, bf16[24,256,1,4,64]{1,4,3,0,2:T(8,128)(2,1)S(1)} %copy-done.7, bf16[24,256,1,4,64]{1,4,3,0,2:T(8,128)(2,1)S(1)} %copy-done.9, bf16[24,256,1,4,64]{1,4,3,0,2:T(8,128)(2,1)S(1)} %copy-done.8), kind=kOutput, calls=%fused_computation.123 | convolution fusion | flops 9673900032 | bytes 23592960 | tf_op jit(solution)/shard_map/btd,btshc->sdhc/dot_general | solution.py:75
  1187.5 99.7 %reduce-scatter.11.cloned.1.call-done = f32[24,64,1024]{2,1,0:T(8,128)} async-done(((f32[24,256,1024]{2,1,0:T(8,128)}), f32[24,64,1024]{2,1,0:T(8,128)}) %reduce-scatter.11.cloned.1.call-update) | async-done | bytes 6291472 | tf_op jit(solution)/shard_map/reduce_scatter | solution.py:77
  1287.3 4.8 convert_reduce_fusion
  1292.1 3.7 fusion.56
  1295.8 3.7 fusion.116
  1299.5 0.6 convert_reduce_fusion.6
  1300.0 4.4 convolution_bitcast_fusion.2
  1304.5 59.5 %all-reduce.2 = (bf16[768,1024]{0,1:T(8,128)(2,1)}, bf16[1024]{0:T(1024)(128)(2,1)}, bf16[2,1024]{1,0:T(2,128)(2,1)}, bf16[2,1024]{1,0:T(2,128)(2,1)}, bf16[1024]{0:T(1024)(128)(2,1)}, /*index=5*/bf16[1024]{0:T(1024)(128)(2,1)}) all-reduce(f32[768,1024]{0,1:T(8,128)} %convolution_bitcast_fusion.2, ...), channel_id=1, replica_groups=mesh['dp'=4,'tp'=4] {'tp'}, use_global_device_ids=true, to_apply=%region_15.0 | all-reduce | flops 793600 | bytes 4761600 | tf_op jit(solution)/shard_map/psum | solution.py:85
  1364.0 2.6 copy.38
  (96 shorter events, 0.3 us)
Async XLA Ops:
  7.2 3.4 copy-start
  7.2 96.4 %all-gather.5.cloned.1.call-start = ((), (), s32[]{:S(2)}) async-start(), calls=%async_computation.4 | async-start | bytes 15728640 | tf_op jit(solution)/shard_map/all_gather | solution.py:29
  8.8 7.8 copy-start.22
  8.9 327.9 %copy-start.24 = (f32[1,1024]{1,0:T(1,128)}, f32[1,1024]{1,0:T(1,128)S(1)}, u32[]{:S(2)}) copy-start(f32[1,1024]{1,0:T(1,128)S(1)} %get-tuple-element.52) | copy-start | bytes 12292
  15.0 1.7 copy-start.1
  15.0 1.7 copy-start.10
  15.0 4.9 copy-start.32
  16.0 0.6 copy-start.18
  16.6 0.6 copy-start.14
  19.7 310.7 %reduce-scatter.5.cloned.1.call-start = ((), (), s32[]{:S(2)}) async-start(), calls=%async_computation.5 | async-start | bytes 31457280 | tf_op jit(solution)/shard_map/reduce_scatter | solution.py:40
  134.1 13.2 copy-start.40
  134.1 13.2 copy-start.37
  159.3 0.7 copy-start.33
  159.3 261.6 %all-gather.7.cloned.1.call-start = ((), (), s32[]{:S(2)}) async-start(), calls=%async_computation.6 | async-start | bytes 15728640 | tf_op jit(solution)/shard_map/all_gather | solution.py:43
  335.1 1.7 copy-start.3
  335.1 1.7 copy-start.12
  336.1 0.6 copy-start.20
  336.8 0.6 copy-start.16
  337.4 3.2 copy-start.34
  339.9 163.3 %all-gather.9.cloned.1.call-start = ((), (), s32[]{:S(2)}) async-start(), calls=%async_computation.8 | async-start | bytes 15728640 | tf_op jit(solution)/shard_map/all_gather | solution.py:52
  340.5 393.1 %reduce-scatter.9.cloned.1.call-start = ((), (), s32[]{:S(2)}) async-start(), calls=%async_computation.9 | async-start | bytes 31457280 | tf_op jit(solution)/shard_map/reduce_scatter | solution.py:60
  340.6 222.0 %copy-start.30 = (f32[1024]{0:T(1024)}, f32[1024]{0:T(1024)S(1)}, u32[]{:S(2)}) copy-start(f32[1024]{0:T(1024)S(1)} %convert_element_type.183) | copy-start | bytes 12292
  503.2 38.2 %copy-start.36 = (bf16[1024,1024]{1,0:T(8,128)(2,1)S(1)}, bf16[1024,1024]{1,0:T(8,128)(2,1)}, u32[]{:S(2)}) copy-start(bf16[1024,1024]{1,0:T(8,128)(2,1)} %param.25) | copy-start | bytes 6291460
  562.5 344.5 %reduce-scatter.7.cloned.1.call-start = ((), (), s32[]{:S(2)}) async-start(), calls=%async_computation.7 | async-start | bytes 31457280 | tf_op jit(solution)/shard_map/reduce_scatter | solution.py:48
  589.3 0.7 copy-start.35
  589.3 144.3 %copy-start.13 = (f32[24,64]{1,0:T(8,128)S(1)}, f32[24,64]{1,0:T(8,128)}, u32[]{:S(2)}) copy-start(f32[24,64]{1,0:T(8,128)} %copy-done.12) | copy-start | bytes 18436
  589.3 144.3 %copy-start.25 = (f32[1,1024]{1,0:T(1,128)S(1)}, f32[1,1024]{1,0:T(1,128)}, u32[]{:S(2)}) copy-start(f32[1,1024]{1,0:T(1,128)} %copy-done.24) | copy-start | bytes 12292
  589.4 409.7 %all-gather.11.cloned.1.call-start = ((), (), s32[]{:S(2)}) async-start(), calls=%async_computation.10 | async-start | bytes 15728640 | tf_op jit(solution)/shard_map/all_gather | solution.py:64
  590.0 149.0 %copy-start.21 = (f32[24,64]{1,0:T(8,128)S(1)}, f32[24,64]{1,0:T(8,128)}, u32[]{:S(2)}) copy-start(f32[24,64]{1,0:T(8,128)} %copy-done.20) | copy-start | bytes 18436
  590.0 149.0 %copy-start.17 = (f32[24,64]{1,0:T(8,128)S(1)}, f32[24,64]{1,0:T(8,128)}, u32[]{:S(2)}) copy-start(f32[24,64]{1,0:T(8,128)} %copy-done.16) | copy-start | bytes 18436
  733.6 5.4 copy-start.4
  739.0 4.3 copy-start.6
  743.3 255.8 %copy-start.38 = (bf16[4,64,1024]{2,1,0:T(8,128)(2,1)S(1)}, bf16[4,64,1024]{2,1,0:T(8,128)(2,1)}, u32[]{:S(2)}) copy-start(bf16[4,64,1024]{2,1,0:T(8,128)(2,1)} %param.23) | copy-start | bytes 1572868
  918.1 95.8 %copy-start.41 = (f32[24,4,256]{2,1,0:T(4,128)S(1)}, f32[24,4,256]{2,1,0:T(4,128)}, u32[]{:S(2)}) copy-start(f32[24,4,256]{2,1,0:T(4,128)} %copy-done.40) | copy-start | bytes 294916
  918.1 369.2 %reduce-scatter.11.cloned.1.call-start = ((), (), s32[]{:S(2)}) async-start(), calls=%async_computation.11 | async-start | bytes 31457280 | tf_op jit(solution)/shard_map/reduce_scatter | solution.py:77
  1116.2 19.1 %copy-start.31 = (f32[1024]{0:T(1024)S(1)}, f32[1024]{0:T(1024)}, u32[]{:S(2)}) copy-start(f32[1024]{0:T(1024)} %copy-done.30) | copy-start | bytes 12292
  1158.3 5.8 copy-start.39
  1164.1 7.7 copy-start.7
  1164.1 7.7 copy-start.8
  1164.1 7.7 copy-start.9
  1171.8 115.4 %copy-start.11 = (f32[24,64]{1,0:T(8,128)S(1)}, f32[24,64]{1,0:T(8,128)}, u32[]{:S(2)}) copy-start(f32[24,64]{1,0:T(8,128)} %copy-done.10) | copy-start | bytes 18436
  1171.8 115.4 %copy-start.23 = (f32[1,1024]{1,0:T(1,128)S(1)}, f32[1,1024]{1,0:T(1,128)}, u32[]{:S(2)}) copy-start(f32[1,1024]{1,0:T(1,128)} %copy-done.22) | copy-start | bytes 12292
  1187.5 104.5 %copy-start.19 = (f32[24,64]{1,0:T(8,128)S(1)}, f32[24,64]{1,0:T(8,128)}, u32[]{:S(2)}) copy-start(f32[24,64]{1,0:T(8,128)} %copy-done.18) | copy-start | bytes 18436
  1187.5 104.6 %copy-start.15 = (f32[24,64]{1,0:T(8,128)S(1)}, f32[24,64]{1,0:T(8,128)}, u32[]{:S(2)}) copy-start(f32[24,64]{1,0:T(8,128)} %copy-done.14) | copy-start | bytes 18436
  1287.3 4.8 copy-start.2
  1292.0 3.8 copy-start.5
  1299.5 5.0 copy-start.26
  1299.5 5.0 copy-start.27
  1299.5 5.0 copy-start.28
  1299.5 5.0 copy-start.29
Sparse Core Ops, SparseCore 0:
  19.8 83.6 all-gather.4
  159.5 170.8 reduce-scatter.4
  340.0 80.8 all-gather.6
  422.3 80.8 all-gather.8
  562.6 170.9 reduce-scatter.8
  736.0 170.8 reduce-scatter.6
  918.2 80.8 all-gather.10
  1116.3 170.8 reduce-scatter.10
where the time goes:
time: 1380 us; the launch traced here: 1370 us
  waiting for transfers between devices  884 us (64%)
  matrix products  354 us (26%)
  blocking collectives  59.5 us (4%)
  other arithmetic  52.6 us (4%)
  between operations  14.8 us (1%)
    reduce_scatter x1, waiting for transfers between devices, group_step(): lax.psum_scatter(attn_part, 'tp', scatter_dimension=1, tiled=True)  170 us
    reduce_scatter x1, waiting for transfers between devices, group_step(): mlp_out = lax.psum_scatter(mlp_part, 'tp', scatter_dimension=1, tiled=True)  164 us
    reduce_scatter x1, waiting for transfers between devices, group_step(): lax.psum_scatter(d_h_two_part, 'tp', scatter_dimension=1, tiled=True)  144 us
    reduce_scatter x1, waiting for transfers between devices, group_step(): lax.psum_scatter(d_h_one_part, 'tp', scatter_dimension=1, tiled=True)  99.7 us
    all_gather x1, waiting for transfers between devices, group_step(): h_one_all = lax.all_gather(h_one_f.astype(half), 'tp', axis=1, tiled=True)  83.6 us
    all_gather x1, waiting for transfers between devices, group_step(): d_x_one_all = lax.all_gather(d_x_one, 'tp', axis=1, tiled=True)  81 us
    all_gather x1, waiting for transfers between devices, group_step(): h_two_all = lax.all_gather(h_two_f.astype(half), 'tp', axis=1, tiled=True)  80.4 us
    all_gather x1, waiting for transfers between devices, group_step(): d_out_all = lax.all_gather(d_out, 'tp', axis=1, tiled=True)  61 us
  transfers between devices with their start and end apart: 8, of which 8 were waited for; matrix products, arithmetic and copies ran while one was open for 9% of the time, Pallas kernels for 0%

commit v1 on v0

v1 whole, which is shorter than its diff:
```python
import jax
import jax.numpy as jnp
from jax import lax
from jax.experimental import pallas as pl
from jax.experimental.pallas import tpu as pltpu
from jax.sharding import PartitionSpec as P

LN_EPS = 1e-6
CORE_PAIRS, X_PAIRS, DIAG_PAIRS = [[(i, i ^ hop) for i in range(4)] for hop in range(1, 4)]
WIDE = jnp.float32
HALF = jnp.bfloat16
LANES = 128
GELU_A = 0.7978845608028654
GELU_B = 0.044715
MLP_TILE = 256


def x_swap(val):
    return lax.ppermute(val, 'tp', X_PAIRS)


def core_swap(val):
    return lax.ppermute(val, 'tp', CORE_PAIRS)


def normalize(x_val):
    centered = x_val - jnp.mean(x_val, axis=-1, keepdims=True)
    row_rstd = lax.rsqrt(jnp.mean(centered * centered, axis=-1, keepdims=True) + LN_EPS)
    return centered * row_rstd, row_rstd


def normalize_back(x_val, scale_f, d_out):
    unit, row_rstd = normalize(x_val)
    d_unit = d_out * scale_f
    inner = d_unit - jnp.mean(d_unit, axis=-1, keepdims=True) - unit * jnp.mean(d_unit * unit, axis=-1, keepdims=True)
    return row_rstd * inner, jnp.sum(d_out * unit, axis=0, keepdims=True), jnp.sum(d_out, axis=0, keepdims=True)


def mm(lhs, rhs):
    return jnp.dot(lhs, rhs, preferred_element_type=WIDE)


def mm_nt(lhs, rhs):
    return lax.dot_general(lhs, rhs, (((1,), (1,)), ((), ())), preferred_element_type=WIDE)


def mm_tn(lhs, rhs):
    return lax.dot_general(lhs, rhs, (((0,), (0,)), ((), ())), preferred_element_type=WIDE)


def run(kernel, grid, in_specs, out_specs, out_shape, flops, scratch=()):
    total = sum(s.size * s.dtype.itemsize for s in jax.tree.leaves(out_shape))
    return pl.pallas_call(
        kernel, grid=(grid,), in_specs=in_specs, out_specs=out_specs, out_shape=out_shape, scratch_shapes=list(scratch),
        cost_estimate=pl.CostEstimate(flops=int(flops), bytes_accessed=2 * total, transcendentals=0),
        compiler_params=pltpu.CompilerParams(dimension_semantics=("arbitrary",)))


def fixed(shape):
    return pl.BlockSpec(shape, lambda i: (0,) * len(shape))


def held(shape):
    return pl.BlockSpec(shape, lambda i: (0,) * len(shape), pipeline_mode=pl.Buffered(1))


def tiled(rows, cols):
    return pl.BlockSpec((rows, cols), lambda i: (i, 0))


STEP = 256


def chunks(size):
    return [slice(col, col + STEP) for col in range(0, size, STEP)]


def first_step(*refs):
    @pl.when(pl.program_id(0) == 0)
    def _():
        for ref in refs:
            ref[...] = jnp.zeros_like(ref)


def shape_of(*dims, dtype=HALF):
    return jax.ShapeDtypeStruct(dims, dtype)


def diag_swap(val):
    return lax.ppermute(val, 'tp', DIAG_PAIRS)


def block(rows, width, at):
    return pl.BlockSpec((rows, width), lambda i: (i, at))


def masks():
    lane = lax.broadcasted_iota(jnp.int32, (1, LANES), 1)
    low = jnp.where(lane < LANES // 2, 1.0, 0.0)
    return low.astype(HALF), (1.0 - low).astype(HALF)


def softmax_cols(keys, query):
    scores = mm_nt(keys, query)
    top = jnp.max(scores, axis=0, keepdims=True)
    weights = jnp.exp((scores - top) * 0.125)
    return weights * (1.0 / jnp.sum(weights, axis=0, keepdims=True))


def split(val, both, axis=0):
    return jnp.concatenate([val * m for m in both], axis=axis)


def rows_of(refs):
    return jnp.concatenate([ref[img] for img in range(refs[0].shape[0]) for ref in refs], axis=0)


def pos_of(ref, dim):
    return jnp.concatenate([ref[0], ref[1][:, :dim - ref.shape[2]]], axis=1).astype(WIDE)


def row_of(ref, first, size):
    used = ref.shape[2] - 512
    parts = [ref[1, first + i:first + i + 1, used:] for i in range(2)]
    return jnp.concatenate(parts, axis=1)[:, :size].astype(WIDE)


def front_kernel(p0_ref, p1_ref, p2_ref, p3_ref, e0_ref, e1_ref, e2_ref, e3_ref,
                 patch_w_ref, patch_b_ref, scale_ref, bias_ref, out_b_ref, w0_ref, w1_ref, w2_ref, w3_ref,
                 emb_ref, qkv_ref, ctx_ref, x_ref, h_ref, pack_ref, acc_ref):
    dim = emb_ref.shape[1]
    width = w0_ref.shape[1] // 4
    both = masks()
    pos = jnp.concatenate([pos_of(ref, dim) for ref in (e0_ref, e1_ref, e2_ref, e3_ref)], axis=0)
    emb = (mm(rows_of((p0_ref, p1_ref, p2_ref, p3_ref)), patch_w_ref[...]) + patch_b_ref[...].astype(WIDE) + pos).astype(HALF)
    emb_ref[...] = emb
    unit, _ = normalize(emb.astype(WIDE))
    h_one = (unit * scale_ref[:1, :].astype(WIDE) + bias_ref[:1, :].astype(WIDE)).astype(HALF)
    pack_ref[:, :dim] = h_one
    for side, w_ref in enumerate((w0_ref, w1_ref, w2_ref, w3_ref)):
        base = 3 * width * side
        bias = row_of((e0_ref, e2_ref, e1_ref, e3_ref)[side], 0, 3 * width)
        for col in range(0, 3 * width, STEP):
            qkv_ref[:, base + col:base + col + STEP] = (mm(h_one, w_ref[:, col:col + STEP]) + bias[:, col:col + STEP]).astype(HALF)
        ctx = []
        for col in range(0, width, LANES):
            query, keys, vals = [qkv_ref[:, base + width * i + col:base + width * i + col + LANES] for i in range(3)]
            probs = jnp.concatenate([softmax_cols(keys, query * m).astype(HALF) for m in both], axis=0)
            ctx.append(mm_tn(split(vals, both), probs).T.astype(HALF))
        ctx = jnp.concatenate(ctx, axis=1)
        to_ref, to = (ctx_ref, width * side) if side < 2 else (pack_ref, 2 * dim + width * (side - 2))
        to_ref[:, to:to + width] = ctx
        part = mm_nt(ctx, w_ref[:, 3 * width:])
        acc_ref[...] = part if side == 0 else acc_ref[...] + part
    x_one = (emb_ref[...].astype(WIDE) + (acc_ref[...] + out_b_ref[...].astype(WIDE))).astype(HALF)
    x_ref[...] = x_one
    unit, _ = normalize(x_one.astype(WIDE))
    h_two = (unit * scale_ref[1:2, :].astype(WIDE) + bias_ref[1:2, :].astype(WIDE)).astype(HALF)
    h_ref[...] = h_two
    pack_ref[:, dim:2 * dim] = h_two


def image_blocks(vals, count=1):
    return [pl.BlockSpec((count,) + val.shape[1:], lambda i: (i, 0, 0)) for val in vals]


def extra_blocks(vals):
    return [pl.BlockSpec((2,) + val.shape[1:], lambda i, at=val.shape[0] // 2 - 1: (at, 0, 0)) for val in vals]


def front(got, patch_w, patch_b, scale, bias, out_b, weights):
    n_own, dim, tile = got[0].shape[0] - 2, patch_w.shape[1], 4 * got[0].shape[1]
    rows = n_own * tile
    outs = [shape_of(rows, dim), shape_of(rows, 3 * dim), shape_of(rows, dim // 2), shape_of(rows, dim), shape_of(rows, dim), shape_of(rows, 2 * dim + dim // 2)]
    vals = (patch_w, patch_b, scale, bias, out_b, *weights)
    return run(front_kernel, n_own, image_blocks(got) + extra_blocks(got) + [held(v.shape) for v in vals], [tiled(tile, o.shape[1]) for o in outs], outs,
               10 * rows * dim * dim, [pltpu.VMEM((tile, dim), WIDE)])(*got, *got, *vals)


def rear_kernel(qkv_ref, dx_ref, emb_ref, p0_ref, p1_ref, p2_ref, p3_ref, scale_ref, w0_ref, w1_ref, w2_ref, w3_ref,
                near_ref, far_ref, patch_ref, pos_ref, sum_ref, qsum_ref, acc_ref):
    first_step(patch_ref, pos_ref, sum_ref, qsum_ref)
    width = w0_ref.shape[1] // 4
    both = masks()
    d_x = dx_ref[...]
    for side, w_ref in enumerate((w0_ref, w1_ref, w2_ref, w3_ref)):
        base = 3 * width * side
        d_ctx_side = mm(d_x, w_ref[:, 3 * width:]).astype(HALF)
        to_ref, to = (near_ref, base) if side < 2 else (far_ref, base - 6 * width)
        for col in range(0, width, LANES):
            query, keys, vals = [qkv_ref[:, base + width * i + col:base + width * i + col + LANES] for i in range(3)]
            d_ctx = d_ctx_side[:, col:col + LANES]
            probs_h, d_scores = [], []
            for m in both:
                probs = softmax_cols(keys, query * m)
                d_probs = mm_nt(vals, d_ctx * m).astype(HALF).astype(WIDE)
                inner = jnp.sum(d_probs * probs, axis=0, keepdims=True)
                d_scores.append((probs * (d_probs - inner) * 0.125).astype(HALF))
                probs_h.append(probs.astype(HALF))
            d_query = mm_tn(split(keys, both), jnp.concatenate(d_scores, axis=0)).T
            d_keys = mm(jnp.concatenate(d_scores, axis=1), split(query, both))
            d_vals = mm(jnp.concatenate(probs_h, axis=1), split(d_ctx, both))
            for i, val in enumerate((d_query, d_keys, d_vals)):
                val_h = val.astype(HALF)
                at = width * i + col
                to_ref[:, to + at:to + at + LANES] = val_h
                qsum_ref[:, base + at:base + at + LANES] += jnp.sum(val_h.astype(WIDE), axis=0, keepdims=True)
        part = mm_nt(to_ref[:, to:to + 3 * width], w_ref[:, :3 * width])
        acc_ref[...] = part if side == 0 else acc_ref[...] + part
    d_h = acc_ref[...].astype(HALF).astype(WIDE)
    d_ln, d_scale, d_bias = normalize_back(emb_ref[...].astype(WIDE), scale_ref[:1, :].astype(WIDE), d_h)
    d_emb = (d_x.astype(WIDE) + d_ln).astype(HALF)
    pos_ref[...] += d_emb.astype(WIDE)
    sum_ref[...] += jnp.concatenate([d_scale, d_bias, jnp.zeros((6, d_emb.shape[1]), WIDE)], axis=0)
    pat = rows_of((p0_ref, p1_ref, p2_ref, p3_ref))
    for rows in chunks(patch_ref.shape[0]):
        patch_ref[rows, :] += mm_tn(pat[:, rows], d_emb)


def rear(qkv, d_x, emb, got, scale, weights):
    rows, dim, tile = emb.shape[0], emb.shape[1], 256
    outs = [shape_of(rows, 3 * dim // 2)] * 2 + [shape_of(got[0].shape[2], dim, dtype=WIDE), shape_of(tile, dim, dtype=WIDE), shape_of(8, dim, dtype=WIDE), shape_of(1, 3 * dim, dtype=WIDE)]
    specs = [tiled(tile, 3 * dim), tiled(tile, dim), tiled(tile, dim)] + image_blocks(got) + [held(scale.shape)] + [held(w.shape) for w in weights]
    return run(rear_kernel, rows // tile, specs, [tiled(tile, 3 * dim // 2)] * 2 + [fixed(o.shape) for o in outs[2:]], outs,
               16 * rows * dim * dim, [pltpu.VMEM((tile, dim), WIDE)])(qkv, d_x, emb, *got, scale, *weights)


def weight_spec(weight):
    val, at = weight
    if val.ndim == 2:
        return held(val.shape)
    return pl.BlockSpec((val.shape[0], 1) + val.shape[2:], lambda i: (0, at, 0, 0), pipeline_mode=pl.Buffered(1))


def w_cols(ref, cols):
    if len(ref.shape) == 2:
        return ref[:, cols]
    return ref[:, 0, :, cols].reshape(ref.shape[0] * ref.shape[2], STEP)


def w_rows(ref, rows):
    if len(ref.shape) == 2:
        return ref[rows, :]
    return ref[rows.start // STEP, 0]


def gelu_both(pre, d_hidden):
    d_hidden = d_hidden.astype(HALF).astype(WIDE)
    square = pre * pre
    bent = jnp.tanh(pre * (GELU_A + (GELU_A * GELU_B) * square))
    cdf = 0.5 + 0.5 * bent
    slope = cdf + pre * (0.5 - 0.5 * bent * bent) * (GELU_A + (3.0 * GELU_A * GELU_B) * square)
    return (pre * cdf).astype(HALF), d_hidden * slope


def up(h_val, d_val, w1_ref, bias, w2_ref, store):
    waiting = None
    for cols in chunks(bias.shape[1]):
        ready = (cols, mm(h_val, w_cols(w1_ref, cols)), mm_nt(d_val, w_rows(w2_ref, cols)))
        if waiting is not None:
            store(waiting[0], *gelu_both(waiting[1] + bias[:, waiting[0]], waiting[2]))
        waiting = ready
    store(waiting[0], *gelu_both(waiting[1] + bias[:, waiting[0]], waiting[2]))


def mlp_kernel(h_ref, x_ref, b2_ref, scale_ref, *refs):
    d_refs, w1_refs, b1_refs, w2_refs = refs[:4], refs[4:8], refs[8:12], refs[12:16]
    own_ref, pack_ref, out_ref, dx_ref, sum_ref, bsum_ref, g_ref, p_ref, acc_ref, dacc_ref = refs[16:]
    first_step(sum_ref, bsum_ref)
    dim = h_ref.shape[1]
    cols_n = g_ref.shape[1]
    d_two = rows_of(d_refs)
    pack_ref[:, 2 * dim:] = d_two
    for side in range(4):
        def store(cols, hidden, d_pre):
            d_pre_h = d_pre.astype(HALF)
            g_ref[:, cols] = hidden
            p_ref[:, cols] = d_pre_h
            shifted = slice(cols_n + cols.start, cols_n + cols.stop)
            if side == 0:
                own_ref[:, cols] = hidden
                own_ref[:, shifted] = d_pre_h
            if side == 2:
                pack_ref[:, cols] = hidden
                pack_ref[:, shifted] = d_pre_h
            if side in (0, 2):
                bsum_ref[side // 2:side // 2 + 1, cols] += jnp.sum(d_pre, axis=0, keepdims=True)

        up(h_ref[...], d_two, w1_refs[side], row_of(b1_refs[side], 2, cols_n), w2_refs[side], store)
        for cols in chunks(dim):
            total = mm(g_ref[...], w_cols(w2_refs[side], cols))
            d_total = mm_nt(p_ref[...], w_rows(w1_refs[side], cols))
            acc_ref[:, cols] = total if side == 0 else acc_ref[:, cols] + total
            dacc_ref[:, cols] = d_total if side == 0 else dacc_ref[:, cols] + d_total
    out_ref[...] = (x_ref[...].astype(WIDE) + (acc_ref[...] + b2_ref[...].astype(WIDE))).astype(HALF)
    d_h = dacc_ref[...].astype(HALF).astype(WIDE)
    d_ln, d_scale, d_bias = normalize_back(x_ref[...].astype(WIDE), scale_ref[1:2, :].astype(WIDE), d_h)
    d_x = (pack_ref[:, 2 * dim:].astype(WIDE) + d_ln).astype(HALF)
    dx_ref[...] = d_x
    sum_ref[...] += jnp.concatenate([d_scale, d_bias, jnp.sum(d_x.astype(WIDE), axis=0, keepdims=True), jnp.zeros((5, dim), WIDE)], axis=0)


def mlp(h_val, d_blocks, x_val, b2, scale, w1s, biases, w2s):
    rows, dim, cols, tile = h_val.shape[0], h_val.shape[1], w2s[0][0].shape[0], MLP_TILE
    specs = [tiled(tile, dim)] * 2 + [held(b2.shape), held(scale.shape)] + image_blocks(d_blocks, tile * d_blocks[0].shape[0] // rows) + [weight_spec(w) for w in w1s] + extra_blocks(biases) + [weight_spec(w) for w in w2s]
    outs = [shape_of(rows, 2 * cols), shape_of(rows, 3 * dim), shape_of(rows, dim), shape_of(rows, dim), shape_of(8, dim, dtype=WIDE), shape_of(8, cols, dtype=WIDE)]
    scratch = [pltpu.VMEM((tile, cols), HALF)] * 2 + [pltpu.VMEM((tile, dim), WIDE)] * 2
    return run(mlp_kernel, rows // tile, specs, [tiled(tile, o.shape[1]) for o in outs[:4]] + [fixed(o.shape) for o in outs[4:]], outs,
               32 * rows * dim * cols, scratch)(h_val, x_val, b2, scale, *d_blocks, *[w[0] for w in w1s], *biases, *[w[0] for w in w2s])


def grad_kernel(la_ref, lb_ref, ra_ref, rb_ref, *out_refs):
    first_step(*out_refs)
    width = out_refs[0].shape[1]
    for rows in chunks(out_refs[0].shape[0]):
        for at, out_ref in enumerate(out_refs):
            cols = slice(width * at, width * (at + 1))
            out_ref[rows, :] += mm_tn(la_ref[:, rows], ra_ref[:, cols]) + mm_tn(lb_ref[:, rows], rb_ref[:, cols])


def grad(ops, count):
    (lhs, dim, _), _, (_, size, _), _ = ops
    rows, tile, width = lhs.shape[0], 512, size // count
    out = shape_of(dim, width, dtype=WIDE)
    return run(grad_kernel, rows // tile, [block(tile, size, at) for _, size, at in ops], [fixed(out.shape)] * count, [out] * count,
               4 * count * rows * dim * width)(*[val for val, _, _ in ops])


def grad_mlp_kernel(ha_ref, ga_ref, da_ref, hb_ref, gb_ref, db_ref, hx_ref, dx_ref, hd_ref, dd_ref, w1_ref, b1_ref, w2_ref,
                    out1_ref, out2_ref, bsum_ref, acc1_ref, acc2_ref, g_ref, p_ref):
    first_step(bsum_ref, acc1_ref, acc2_ref)
    cols_n = w1_ref.shape[1]
    for at, (h_ref, d_ref) in enumerate(((hx_ref, dx_ref), (hd_ref, dd_ref))):
        def store(cols, hidden, d_pre):
            g_ref[at, :, cols] = hidden
            p_ref[at, :, cols] = d_pre.astype(HALF)
            bsum_ref[:, cols] += jnp.sum(d_pre, axis=0, keepdims=True)

        up(h_ref[...], d_ref[...], w1_ref, b1_ref[...].astype(WIDE), w2_ref, store)
    for rows in chunks(acc1_ref.shape[0]):
        acc1_ref[rows, :] += mm_tn(ha_ref[:, rows], ga_ref[:, cols_n:]) + mm_tn(hb_ref[:, rows], gb_ref[:, cols_n:]) + mm_tn(hx_ref[:, rows], p_ref[0]) + mm_tn(hd_ref[:, rows], p_ref[1])
    for rows in chunks(acc2_ref.shape[0]):
        acc2_ref[rows, :] += mm_tn(ga_ref[:, rows], da_ref[...]) + mm_tn(gb_ref[:, rows], db_ref[...]) + mm_tn(g_ref[0, :, rows], dx_ref[...]) + mm_tn(g_ref[1, :, rows], dd_ref[...])

    @pl.when(pl.program_id(0) == pl.num_programs(0) - 1)
    def _():
        out1_ref[...] = acc1_ref[...].astype(HALF)
        out2_ref[...] = acc2_ref[...].astype(HALF)


def grad_mlp(ops, w1, b1, w2):
    rows, (dim, cols), tile = ops[0][0].shape[0], w1.shape, 256
    outs = [shape_of(dim, cols), shape_of(cols, dim), shape_of(1, cols, dtype=WIDE)]
    scratch = [pltpu.VMEM((dim, cols), WIDE), pltpu.VMEM((cols, dim), WIDE)] + [pltpu.VMEM((2, tile, cols), HALF)] * 2
    return run(grad_mlp_kernel, rows // tile, [block(tile, width, at) for _, width, at in ops] + [held(w1.shape), held(b1.shape), held(w2.shape)],
               [fixed(o.shape) for o in outs], outs, 24 * rows * dim * cols, scratch)(*[val for val, _, _ in ops], w1, b1, w2)


def gather_pieces(piece):
    group = lax.axis_index('dp')
    pieces = [(x_swap(piece), group)]
    for hop, at in enumerate((group + 1 - 2 * (group % 2), (group + 2) % 4, 3 - group), 1):
        pieces.append((lax.ppermute(pieces[0][0], 'dp', [(i, i ^ hop) for i in range(4)]), at))
    return pieces


def after(vals, done):
    return lax.optimization_barrier((vals, done))[0]


def group_step(patches, patch_w, patch_b, pos_emb, ln_scale, ln_bias, qkv_w, qkv_b, out_w, out_b, fc1_w, fc1_b, fc2_w, fc2_b, d_out):
    n_img, n_tok, patch_dim = patches.shape
    dim = patch_w.shape[1]
    n_own = n_img // 4
    rows = n_own * 4 * n_tok
    cols = fc1_w.shape[1]
    group, me = lax.axis_index('dp'), lax.axis_index('tp')
    core = me % 2
    core_set = me + 1 - 2 * core
    sets = (me, core_set, (me + 2) % 4, (core_set + 2) % 4)

    def images(val, which):
        return lax.dynamic_slice_in_dim(val, sets[which] * n_own, n_own, 0)

    def quarter(val):
        part = val.shape[0] // 4
        return lax.dynamic_slice_in_dim(val, group * part, part, 0)

    row = lambda val: val.reshape(1, val.shape[-1])

    heads = qkv_w.shape[2] * qkv_w.shape[3]
    attn_w = jnp.concatenate([jnp.swapaxes(qkv_w, 0, 1).reshape(dim, 3 * heads), out_w.reshape(heads, dim).T], axis=1)
    attn_pieces = gather_pieces(quarter(attn_w))
    flat = jnp.concatenate([qkv_b.reshape(3 * heads), jnp.zeros((1024 - 3 * heads,), HALF), fc1_b]).reshape(4, 512)
    beside = jnp.concatenate([pos_emb[:, patch_dim:], jnp.pad(flat, ((0, n_tok - 4), (0, 0)))], axis=1)
    extra = jnp.stack([pos_emb[:, :patch_dim], beside])
    with_extra = lambda which: jnp.concatenate([images(patches, which), extra], axis=0)
    got = (with_extra(0), core_swap(with_extra(1)), x_swap(with_extra(2)), diag_swap(with_extra(3)))
    mlp_pieces = gather_pieces(jnp.stack([quarter(fc1_w), quarter(fc2_w)]))
    d_blocks = (images(d_out, 0), core_swap(images(d_out, 1)), x_swap(images(d_out, 2)), diag_swap(images(d_out, 3)))
    attn_c = core_swap(attn_w)
    fc1_c, fc2_c = core_swap(fc1_w), core_swap(fc2_w)

    attn_x = jnp.zeros_like(attn_w)
    for val, at in attn_pieces:
        attn_x = lax.dynamic_update_slice(attn_x, val, (at * (dim // 4), 0))
    attn_d = core_swap(attn_x)
    mlp_x = jnp.zeros((4, 2, dim // 4, cols), HALF)
    for val, at in mlp_pieces:
        mlp_x = lax.dynamic_update_slice(mlp_x, val[None], (at, 0, 0, 0))
    mlp_d = core_swap(mlp_x)
    attn_ws = (attn_w, attn_x, attn_c, attn_d)

    emb, qkv, ctx, x_one, h_two, pack_f = front(got, patch_w, row(patch_b), ln_scale, ln_bias, row(out_b), attn_ws)
    h_two_x = x_swap(h_two)
    pack_f_c = core_swap(pack_f)
    h_two_d = core_swap(h_two_x)

    w1s, w2s = ((fc1_w, 0), (mlp_x, 0), (fc1_c, 0), (mlp_d, 0)), ((fc2_w, 0), (mlp_x, 1), (fc2_c, 0), (mlp_d, 1))
    own_gp, pack_m, x_two, d_x, sums_two, b_sums = mlp(h_two, d_blocks, x_one, row(fc2_b), ln_scale, w1s, (got[0], got[2], got[1], got[3]), w2s)
    pack_m_c = core_swap(pack_m)
    x_blocks = x_two.reshape(n_own, 4, n_tok, dim)
    x_parts = (x_blocks[:, 0], core_swap(x_blocks[:, 1]), x_swap(x_blocks[:, 2]), diag_swap(x_blocks[:, 3]))
    d_x_c = core_swap(d_x)
    d_o_own, d_o_x = grad(((d_x, dim, 0), (d_x_c, dim, 0), (ctx, 2 * heads, 0), (pack_f_c, 2 * heads, 4)), 2)
    d_o_recv = x_swap(d_o_x)
    d_near, d_far, d_patch_part, d_pos_all, sums_one, d_qkv_sum = rear(qkv, d_x, emb, got, ln_scale, attn_ws)
    d_far_c = core_swap(d_far)
    third = 3 * heads
    d_qkv_x, = grad(((pack_f, dim, 0), (pack_f_c, dim, 0), (d_near, third, 1), (d_far_c, third, 1)), 1)
    d_qkv_recv = x_swap(d_qkv_x)
    d_qkv_own, = grad(((pack_f, dim, 0), (pack_f_c, dim, 0), (d_near, third, 0), (d_far_c, third, 0)), 1)

    def in_order(flip, low, high):
        return jnp.where(flip == 0, jnp.concatenate([low, high], axis=0), jnp.concatenate([high, low], axis=0))

    x_parts = after(x_parts, d_qkv_x)
    x_two_out = in_order(me // 2, in_order(core, x_parts[0], x_parts[1]), in_order(core, x_parts[2], x_parts[3]))

    d_parts = (x_swap(images(d_out, 0)), diag_swap(images(d_out, 1)), images(d_out, 2), core_swap(images(d_out, 3)))
    d_oth = jnp.concatenate(after(d_parts, d_qkv_x), axis=1).reshape(rows, dim)
    d_oth_d = core_swap(d_oth)
    d_fc1_w, d_fc2_w, sum_other = grad_mlp((
        (h_two, dim, 0), (own_gp, 2 * cols, 0), (pack_m, dim, 2), (pack_f_c, dim, 1), (pack_m_c, 2 * cols, 0), (pack_m_c, dim, 2),
        (h_two_x, dim, 0), (d_oth, dim, 0), (h_two_d, dim, 0), (d_oth_d, dim, 0)), fc1_w, row(fc1_b), fc2_w)
    d_fc2_b = jnp.sum(d_out, axis=(0, 1), dtype=WIDE)

    half_rows = patch_dim // 2
    mine = lax.dynamic_slice_in_dim(d_patch_part, core * half_rows, half_rows, 0)
    theirs = lax.dynamic_slice_in_dim(d_patch_part, (1 - core) * half_rows, half_rows, 0)
    mine = mine + core_swap(theirs)
    mine = (mine + x_swap(mine)).astype(HALF)
    theirs = core_swap(mine)
    d_patch_w = jnp.where(core == 0, jnp.concatenate([mine, theirs]), jnp.concatenate([theirs, mine]))

    d_pos_all, d_qkv_sum, sums_one = after((d_pos_all, d_qkv_sum, sums_one), d_qkv_x)
    d_patch_b = jnp.sum(d_pos_all, axis=0, keepdims=True)
    small = jnp.concatenate([sums_one[:1], sums_two[:1], sums_one[1:2], sums_two[1:2], sums_two[2:3], d_patch_b, row(d_fc2_b)], axis=0)
    wide_row = lambda side: jnp.pad(d_qkv_sum[:, 3 * heads * side:3 * heads * (side + 1)], ((0, 0), (0, dim - 3 * heads)))
    pos_block = lambda at: d_pos_all[at * n_tok:(at + 1) * n_tok]
    from_core = core_swap(jnp.concatenate([pos_block(1), pos_block(3), small, wide_row(2), wide_row(3), b_sums[1:2]], axis=0))
    mine_sum = jnp.concatenate([pos_block(0), pos_block(2), small, wide_row(0), wide_row(1), b_sums[:1]], axis=0) + from_core
    d_fc1_b = mine_sum[2 * n_tok + 9] + sum_other[0]
    small = mine_sum[2 * n_tok:2 * n_tok + 7]
    from_x = x_swap(jnp.concatenate([mine_sum[n_tok:2 * n_tok], small, mine_sum[2 * n_tok + 8:2 * n_tok + 9]], axis=0))
    total = (jnp.concatenate([mine_sum[:n_tok], small, mine_sum[2 * n_tok + 7:2 * n_tok + 8]], axis=0) + from_x).astype(HALF)
    d_pos, small, d_qkv_b = total[:n_tok], total[n_tok:n_tok + 7], total[n_tok + 7, :3 * heads]

    d_qkv_w = jnp.swapaxes((d_qkv_own + d_qkv_recv).astype(HALF).reshape((dim,) + qkv_b.shape), 0, 1)
    d_out_w = (d_o_own + d_o_recv).astype(HALF).T.reshape(out_w.shape)
    return (x_two_out, d_patch_w, small[5], d_pos, small[:2], small[2:4], d_qkv_w, d_qkv_b.reshape(qkv_b.shape), d_out_w, small[4], d_fc1_w, d_fc1_b.astype(HALF), d_fc2_w, small[6])


def solution(mesh):
    in_specs = (P('dp', 'tp'), P(), P(), P('tp'), P(), P(), P(None, None, 'tp'), P(None, 'tp'), P('tp'), P(), P(None, 'tp'), P('tp'), P('tp'), P(), P('dp', 'tp'))
    out_specs = (P('dp', 'tp'), P('dp'), P('dp'), P(('dp', 'tp')), P('dp'), P('dp'), P('dp', None, 'tp'), P('dp', 'tp'), P(('dp', 'tp')), P('dp'), P('dp', 'tp'), P(('dp', 'tp')), P(('dp', 'tp')), P('dp'))
    return jax.shard_map(group_step, mesh=mesh, in_specs=in_specs, out_specs=out_specs, check_vma=False)
```

time: 1380 us -> 680 us (0.49)
  waiting for transfers between devices: 884 us -> 301 us
  matrix products: 354 us -> 0 us
  Pallas kernels: 0 us -> 270 us
  blocking collectives: 59.5 us -> 0 us
  local copies, waits for them, and re-layouts: 7.62 us -> 44.5 us
  starting transfers between devices: 0.71 us -> 26.6 us
  other arithmetic: 52.6 us -> 28.5 us
    reduce_scatter x4 -> x0, waiting for transfers between devices: 577 us -> none  [the longest x1 170 us: group_step(): lax.psum_scatter(attn_part, 'tp', scatter_dimension=1, tiled=True)]
    dot_general x19 -> x0, matrix products: 339 us -> none  [the longest x1 38.2 us: group_step(): jnp.einsum('btd,fd->btf', d_out_all, fc2_w, preferred_element_type=wide)]
    all_gather x4 -> x0, waiting for transfers between devices: 306 us -> none  [the longest x1 83.6 us: group_step(): h_one_all = lax.all_gather(h_one_f.astype(half), 'tp', axis=1, tiled=True)]
    ppermute x0 -> x39, waiting for transfers between devices: none -> 301 us  [the longest x11 215 us: x_swap(): return lax.ppermute(val, 'tp', X_PAIRS)]
    pallas_call x0 -> x7, Pallas kernels: none -> 270 us  [the longest x1 73.7 us: mlp(): run(mlp_kernel, rows // tile, specs, [tiled(tile, o.shape[1]) for o in ou...]
    psum x1 -> x0, blocking collectives: 59.5 us -> none  [group_step(): lax.psum((d_patch_w, d_patch_b, d_ln_scale, d_ln_bias, d_out_b, d_fc2_b),...]
    reduce_sum x11 -> x2, other arithmetic: 45.8 us -> 0.67 us  [the longest x1 0.59 us: group_step(): d_fc2_b = jnp.sum(d_out, axis=(0, 1), dtype=WIDE)]
    ppermute x0 -> x39, starting transfers between devices: none -> 26.6 us  [the longest x11 12.1 us: x_swap(): return lax.ppermute(val, 'tp', X_PAIRS)]
  transfers between devices with their start and end apart: 8 -> 39, of which waited for: 8 -> 14; matrix products, arithmetic and copies ran while one was open for 9% -> 10% of each run, Pallas kernels for 0% -> 32%
where the time goes in v1:
time: 680 us; the launch traced here: 672 us
  waiting for transfers between devices  301 us (44%)
  Pallas kernels  270 us (40%)
  local copies, waits for them, and re-layouts  44.5 us (7%)
  other arithmetic  28.5 us (4%)
  starting transfers between devices  26.6 us (4%)
    ppermute x11, waiting for transfers between devices, x_swap(): return lax.ppermute(val, 'tp', X_PAIRS)  215 us
    pallas_call x1, Pallas kernels, mlp(): run(mlp_kernel, rows // tile, specs, [tiled(tile, o.shape[1]) for o in ou...  73.7 us
    pallas_call x1, Pallas kernels, rear(): run(rear_kernel, rows // tile, specs, [tiled(tile, 3 * dim // 2)] * 2 + [...  64.8 us
    pallas_call x1, Pallas kernels, front(): run(front_kernel, n_own, image_blocks(got) + extra_blocks(got) + [held(v....  52.3 us
    pallas_call x1, Pallas kernels, grad_mlp(): run(grad_mlp_kernel, rows // tile, [block(tile, width, at) for _, width,...  51.5 us
    ppermute x4, waiting for transfers between devices, diag_swap(): return lax.ppermute(val, 'tp', DIAG_PAIRS)  45.8 us
    ppermute x6, waiting for transfers between devices, gather_pieces(): lax.ppermute(pieces[0][0], 'dp', [(i, i ^ hop) for i in range(4)])  40.4 us
    pallas_call x3, Pallas kernels, grad(): run(grad_kernel, rows // tile, [block(tile, size, at) for _, size, at in...  27.4 us
  transfers between devices with their start and end apart: 39, of which 14 were waited for; matrix products, arithmetic and copies ran while one was open for 10% of the time, Pallas kernels for 32%

profile of v1, /device:TPU:0, one launch (start us, length us, event | category | flops | bytes accessed | tf_op | source)
XLA Modules:
  0.0 671.7 jit_solution(13683130096578934918)
XLA Ops:
  0.7 1.1 dynamic-slice_bitcast_fusion
  1.8 1.1 dynamic-slice_bitcast_fusion.1
  2.9 1.1 pad_maximum_fusion.10
  3.9 3.2 collective-permute-start.12
  7.4 1.8 copy.38
  9.2 21.3 %collective-permute-done.12 = bf16[2,256,1024]{2,1,0:T(8,128)(2,1)S(1)} collective-permute-done((bf16[2,256,1024]{2,1,0:T(8,128)(2,1)}, bf16[2,256,1024]{2,1,0:T(8,128)(2,1)S(1)}, u32[]{:S(2)}, u32[]{:S(2)}) %collective-permute-start.12) | collective-permute-done | bytes 1048608 | tf_op jit(solution)/shard_map/ppermute | solution.py:19
  30.5 1.8 collective-permute-start.13
  33.1 1.5 collective-permute-start.3
  34.8 1.6 collective-permute-start.14
  36.8 1.8 constant_dynamic-slice_fusion.5
  38.7 1.8 pad_maximum_fusion.2
  40.4 5.5 collective-permute-done.3
  46.5 2.5 broadcast_in_dim.26
  49.0 1.0 bitcast_dynamic-update-slice_fusion.3
  50.0 6.6 collective-permute-done.13
  56.6 1.8 collective-permute-start.5
  58.5 2.3 bitcast_dynamic-update-slice_fusion.2
  60.8 22.6 %collective-permute-done.14 = bf16[2,256,1024]{2,1,0:T(8,128)(2,1)} collective-permute-done((bf16[2,256,1024]{2,1,0:T(8,128)(2,1)S(1)}, bf16[2,256,1024]{2,1,0:T(8,128)(2,1)}, u32[]{:S(2)}, u32[]{:S(2)}) %collective-permute-start.14) | collective-permute-done | bytes 1048608 | tf_op jit(solution)/shard_map/ppermute | solution.py:363
  83.4 1.5 collective-permute-start.6
  84.9 2.3 bitcast_dynamic-update-slice_fusion.1
  87.2 2.3 bitcast_dynamic-update-slice_fusion.refs_5_.refs_13_
  90.1 1.8 constant_dynamic-update-slice_fusion.3
  92.1 11.1 %collective-permute-done.5 = bf16[256,1024]{1,0:T(8,128)(2,1)S(1)} collective-permute-done((bf16[256,1024]{1,0:T(8,128)(2,1)}, bf16[256,1024]{1,0:T(8,128)(2,1)S(1)}, u32[]{:S(2)}, u32[]{:S(2)}) %collective-permute-start.5) | collective-permute-done | bytes 524320 | tf_op jit(solution)/shard_map/ppermute | solution.py:363
  104.0 1.5 constant_dynamic-slice_fusion.1
  106.1 6.3 collective-permute-done.1.p2_ref.e2_ref.refs_9_
  112.4 15.9 %collective-permute-done.2.p3_ref.e3_ref.refs_11_ = bf16[8,64,768]{2,1,0:T(8,128)(2,1)S(1)} collective-permute-done((bf16[8,64,768]{2,1,0:T(8,128)(2,1)S(1)}, bf16[8,64,768]{2,1,0:T(8,128)(2,1)S(1)}, u32[]{:S(2)}, u32[]{:S(2)}) %collective-permute-start.2) | collective-permute-done | bytes 786464 | tf_op jit(solution)/shard_map/ppermute | solution.py:90
  131.8 0.9 copy-done.30
  133.3 52.3 %shard_map.254 = (bf16[1536,1024]{1,0:T(8,128)(2,1)}, bf16[1536,3072]{1,0:T(8,128)(2,1)}, bf16[1536,512]{1,0:T(8,128)(2,1)}, bf16[1536,1024]{1,0:T(8,128)(2,1)},...) custom-call(bf16[8,64,768]{2,1,0:T(8,128)(2,1)} %get-tuple-element.118.p0_ref.e0_ref.refs_8_, ...), custom_call_target="tpu_custom_call" | custom-call | flops 16106127360 | bytes 56623104 | tf_op jit(solution)/shard_map/pallas_call | solution.py:176
  185.9 73.7 %shard_map.255 = (bf16[1536,2048]{1,0:T(8,128)(2,1)}, bf16[1536,3072]{1,0:T(8,128)(2,1)}, bf16[1536,1024]{1,0:T(8,128)(2,1)}, bf16[1536,1024]{1,0:T(8,128)(2,1)}, f32[8,1024]{1,0:T(8,128)}, /*index=5*/f32[8,1024]{1,0:T(8,128)}) custom-call(bf16[1536,1024]{1,0:T(8,128)(2,1)} %get-tuple-element.48.h_ref.ha_ref, bf16[1536,1024]{1,0:T(8,128)(2,1)} %get-tuple-element.49.x_ref, ...), custom_call_target="tpu_custom_call" | custom-call | flops 51539607552 | bytes 44171264 | tf_op jit(solution)/shard_map/pallas_call | solution.py:308
  259.6 64.8 %shard_map.256 = (bf16[1536,1536]{1,0:T(8,128)(2,1)}, bf16[1536,1536]{1,0:T(8,128)(2,1)}, f32[768,1024]{1,0:T(8,128)}, f32[256,1024]{1,0:T(8,128)}, f32[8,1024]{1,0:T(8,128)}, /*index=5*/f32[1,3072]{1,0:T(1,128)}) custom-call(bf16[1536,3072]{1,0:T(8,128)(2,1)} %get-tuple-element.52.qkv_ref, bf16[1536,1024]{1,0:T(8,128)(2,1)} %get-tuple-element.53.dx_ref.la_ref, ...), custom_call_target="tpu_custom_call" | custom-call | flops 25769803776 | bytes 27353088 | tf_op jit(solution)/shard_map/pallas_call | solution.py:224
  324.9 1.3 collective-permute-start.34
  326.2 1.6 constant_dynamic-slice_fusion
  327.9 17.0 %collective-permute-done.34 = bf16[6,64,1024]{2,1,0:T(8,128)(2,1)} collective-permute-done((bf16[6,64,1024]{2,1,0:T(8,128)(2,1)}, bf16[6,64,1024]{2,1,0:T(8,128)(2,1)}, u32[]{:S(2)}, u32[]{:S(2)}) %collective-permute-start.34) | collective-permute-done | bytes 786464 | tf_op jit(solution)/shard_map/ppermute | solution.py:19
  345.4 19.3 %collective-permute-done.35 = bf16[6,64,1024]{2,1,0:T(8,128)(2,1)S(1)} collective-permute-done((bf16[6,64,1024]{2,1,0:T(8,128)(2,1)S(1)}, bf16[6,64,1024]{2,1,0:T(8,128)(2,1)S(1)}, u32[]{:S(2)}, u32[]{:S(2)}) %collective-permute-start.35) | collective-permute-done | bytes 786464 | tf_op jit(solution)/shard_map/ppermute | solution.py:90
  365.6 1.1 collective-permute-start.33
  366.8 2.1 dynamic-slice_add_fusion
  368.9 0.9 collective-permute-start.25
  370.8 1.4 slice_bitcast_fusion
  372.2 97.4 %collective-permute-done.25 = f32[384,1024]{1,0:T(8,128)S(1)} collective-permute-done((f32[384,1024]{1,0:T(8,128)S(1)}, f32[384,1024]{1,0:T(8,128)S(1)}, u32[]{:S(2)}, u32[]{:S(2)}) %collective-permute-start.25) | collective-permute-done | bytes 1572896 | tf_op jit(solution)/shard_map/ppermute | solution.py:19
  470.1 1.4 fusion.10
  473.5 0.9 collective-permute-start.20
  474.4 9.9 %shard_map.257 = f32[1024,768]{1,0:T(8,128)} custom-call(bf16[1536,2560]{1,0:T(8,128)(2,1)} %get-tuple-element.51.la_ref, bf16[1536,2560]{1,0:T(8,128)(2,1)} %collective-permute-done.22.lb_ref.rb_ref.hb_ref, bf16[1536,1536]{1,0:T(8,128)(2,1)} %get-tuple-element.55.ra_ref, bf16[1536,1536]{1,0:T(8,128)(2,1)} %collective-permute-done.23.rb_ref), custom_call_target="tpu_custom_call" | custom-call | flops 4831838208 | bytes 6291456 | tf_op jit(solution)/shard_map/pallas_call | solution.py:325
  487.4 3.8 concatenate.87
  491.2 3.1 collective-permute-done.20
  495.7 3.2 maximum_select_fusion.3
  498.9 10.6 %collective-permute-done.21 = bf16[6,64,1024]{2,1,0:T(8,128)(2,1)} collective-permute-done((bf16[6,64,1024]{2,1,0:T(8,128)(2,1)}, bf16[6,64,1024]{2,1,0:T(8,128)(2,1)}, u32[]{:S(2)}, u32[]{:S(2)}) %collective-permute-start.21) | collective-permute-done | bytes 786464 | tf_op jit(solution)/shard_map/ppermute | solution.py:90
  509.5 1.5 collective-permute-start.37
  510.9 3.1 pad_maximum_fusion
  514.2 2.1 maximum_select_fusion.2
  516.3 9.6 %shard_map.258 = f32[1024,768]{1,0:T(8,128)} custom-call(bf16[1536,2560]{1,0:T(8,128)(2,1)} %get-tuple-element.51.la_ref, bf16[1536,2560]{1,0:T(8,128)(2,1)} %collective-permute-done.22.lb_ref.rb_ref.hb_ref, bf16[1536,1536]{1,0:T(8,128)(2,1)} %get-tuple-element.55.ra_ref, bf16[1536,1536]{1,0:T(8,128)(2,1)} %collective-permute-done.23.rb_ref), custom_call_target="tpu_custom_call" | custom-call | flops 4831838208 | bytes 6291456 | tf_op jit(solution)/shard_map/pallas_call | solution.py:325
  525.9 1.1 add.146
  527.1 0.9 collective-permute-start.28
  528.0 7.8 %shard_map.259 = (f32[1024,256]{1,0:T(8,128)}, f32[1024,256]{1,0:T(8,128)}) custom-call(bf16[1536,1024]{1,0:T(8,128)(2,1)} %get-tuple-element.53.dx_ref.la_ref, bf16[1536,1024]{1,0:T(8,128)(2,1)} %collective-permute-done.30.lb_ref, bf16[1536,512]{1,0:T(8,128)(2,1)} %get-tuple-element.70.ra_ref, bf16[1536,2560]{1,0:T(8,128)(2,1)} %collective-permute-done.22.lb_ref.rb_ref.hb_ref), custom_call_target="tpu_custom_call" | custom-call | flops 3221225472 | bytes 4194304 | tf_op jit(solution)/shard_map/pallas_call | solution.py:325
  535.8 47.9 %collective-permute-done.28 = f32[72,1024]{1,0:T(8,128)S(1)} collective-permute-done((f32[72,1024]{1,0:T(8,128)S(1)}, f32[72,1024]{1,0:T(8,128)S(1)}, u32[]{:S(2)}, u32[]{:S(2)}) %collective-permute-start.28) | collective-permute-done | bytes 294944 | tf_op jit(solution)/shard_map/ppermute | solution.py:19
  584.6 1.6 maximum_select_fusion.1
  586.2 1.9 maximum_select_fusion
  588.2 1.2 fusion.2
  592.0 16.3 %collective-permute-done.31 = f32[1024,256]{1,0:T(8,128)} collective-permute-done((f32[1024,256]{1,0:T(8,128)}, f32[1024,256]{1,0:T(8,128)}, u32[]{:S(2)}, u32[]{:S(2)}) %collective-permute-start.31) | collective-permute-done | bytes 1048608 | tf_op jit(solution)/shard_map/ppermute | solution.py:19
  608.3 2.4 fusion
  610.7 2.0 copy.44
  612.8 3.3 add_convert_fusion
  616.1 2.6 copy.43
  618.7 51.5 %shard_map.260 = (bf16[1024,1024]{1,0:T(8,128)(2,1)}, bf16[1024,1024]{1,0:T(8,128)(2,1)}, f32[1,1024]{1,0:T(1,128)}) custom-call(bf16[1536,1024]{1,0:T(8,128)(2,1)} %get-tuple-element.48.h_ref.ha_ref, bf16[1536,2048]{1,0:T(8,128)(2,1)} %get-tuple-element.73.ga_ref, bf16[1536,3072]{1,0:T(8,128)(2,1)} %get-tuple-element.74.da_ref, ...), custom_call_target="tpu_custom_call" | custom-call | flops 38654705664 | bytes 8396800 | tf_op jit(solution)/shard_map/pallas_call | solution.py:355
  670.2 1.4 fusion.7
  (162 shorter events, 22.1 us)
Async XLA Ops:
  0.6 6.5 copy-start.13
  3.9 26.6 %collective-permute-start.12 = (bf16[2,256,1024]{2,1,0:T(8,128)(2,1)}, bf16[2,256,1024]{2,1,0:T(8,128)(2,1)S(1)}, u32[]{:S(2)}, u32[]{:S(2)}) collective-permute-start(bf16[2,256,1024]{2,1,0:T(8,128)(2,1)} %pad_maximum_fusion.10), channel_id=1, source_target_pairs={{0,2},{1,3},{2,0},{3,1},{4,6},{5,7},{6,4},{7,5},{8,10},{9,11},{10,... | collective-permute-start | bytes 3145736 | tf_op jit(solution)/shard_map/ppermute | solution.py:19
  7.4 27.3 %copy-start.26 = (bf16[3,4,64]{2,1,0:T(4,128)(2,1)S(1)}, bf16[3,4,64]{2,1,0:T(4,128)(2,1)}, u32[]{:S(2)}) copy-start(bf16[3,4,64]{2,1,0:T(4,128)(2,1)} %param.22) | copy-start | bytes 4612
  7.4 27.4 %copy-start.24 = (bf16[1024]{0:T(1024)(128)(2,1)S(1)}, bf16[1024]{0:T(1024)(128)(2,1)}, u32[]{:S(2)}) copy-start(bf16[1024]{0:T(1024)(128)(2,1)} %param.26) | copy-start | bytes 6148
  7.4 29.0 %copy-start.15 = (bf16[64,1024]{1,0:T(8,128)(2,1)S(1)}, bf16[64,1024]{1,0:T(8,128)(2,1)}, u32[]{:S(2)}) copy-start(bf16[64,1024]{1,0:T(8,128)(2,1)} %param.18) | copy-start | bytes 393220
  7.4 29.0 %slice-start = ((bf16[64,1024]{1,0:T(8,128)(2,1)}), bf16[64,256]{1,0:T(8,128)(2,1)S(1)}, s32[]{:S(2)}) async-start(bf16[64,1024]{1,0:T(8,128)(2,1)} %param.18), calls=%async_computation | async-start | bytes 65536 | tf_op jit(solution)/shard_map/slice | solution.py:395
  30.5 26.1 %collective-permute-start.13 = (bf16[2,256,1024]{2,1,0:T(8,128)(2,1)S(1)}, bf16[2,256,1024]{2,1,0:T(8,128)(2,1)}, u32[]{:S(2)}, u32[]{:S(2)}) collective-permute-start(bf16[2,256,1024]{2,1,0:T(8,128)(2,1)S(1)} %collective-permute-done.12), channel_id=1, source_target_pairs={{0,4},{4,0},{8,12},{12,8},{1,5},{5,1},{9,13},{13,9},{2,6},{6,2},{1... | collective-permute-start | bytes 3145736 | tf_op jit(solution)/shard_map/ppermute | solution.py:363
  33.1 12.8 %collective-permute-start.3 = (bf16[256,1024]{1,0:T(8,128)(2,1)}, bf16[256,1024]{1,0:T(8,128)(2,1)}, u32[]{:S(2)}, u32[]{:S(2)}) collective-permute-start(bf16[256,1024]{1,0:T(8,128)(2,1)} %fusion.1), channel_id=1, source_target_pairs={{0,2},{1,3},{2,0},{3,1},{4,6},{5,7},{6,4},{7,5},{8,10},{9,11},{10,... | collective-permute-start | bytes 1572872 | tf_op jit(solution)/shard_map/ppermute | solution.py:19
  34.8 48.6 %collective-permute-start.14 = (bf16[2,256,1024]{2,1,0:T(8,128)(2,1)S(1)}, bf16[2,256,1024]{2,1,0:T(8,128)(2,1)}, u32[]{:S(2)}, u32[]{:S(2)}) collective-permute-start(bf16[2,256,1024]{2,1,0:T(8,128)(2,1)S(1)} %collective-permute-done.12), channel_id=1, source_target_pairs={{0,8},{4,12},{8,0},{12,4},{1,9},{5,13},{9,1},{13,5},{2,10},{6,14},... | collective-permute-start | bytes 3145736 | tf_op jit(solution)/shard_map/ppermute | solution.py:363
  36.4 50.8 %collective-permute-start.15 = (bf16[2,256,1024]{2,1,0:T(8,128)(2,1)S(1)}, bf16[2,256,1024]{2,1,0:T(8,128)(2,1)}, u32[]{:S(2)}, u32[]{:S(2)}) collective-permute-start(bf16[2,256,1024]{2,1,0:T(8,128)(2,1)S(1)} %collective-permute-done.12), channel_id=1, source_target_pairs={{0,12},{4,8},{8,4},{12,0},{1,13},{5,9},{9,5},{13,1},{2,14},{6,10},... | collective-permute-start | bytes 3145736 | tf_op jit(solution)/shard_map/ppermute | solution.py:363
  40.4 65.1 %collective-permute-start = (bf16[8,64,768]{2,1,0:T(8,128)(2,1)}, bf16[8,64,768]{2,1,0:T(8,128)(2,1)}, u32[]{:S(2)}, u32[]{:S(2)}) collective-permute-start(bf16[8,64,768]{2,1,0:T(8,128)(2,1)} %get-tuple-element.116), channel_id=1, source_target_pairs={{0,1},{1,0},{2,3},{3,2},{4,5},{5,4},{6,7},{7,6},{8,9},{9,8},{10,11... | collective-permute-start | bytes 2359304 | tf_op jit(solution)/shard_map/ppermute | solution.py:23
  46.0 45.9 %collective-permute-start.4 = (bf16[256,1024]{1,0:T(8,128)(2,1)}, bf16[256,1024]{1,0:T(8,128)(2,1)S(1)}, u32[]{:S(2)}, u32[]{:S(2)}) collective-permute-start(bf16[256,1024]{1,0:T(8,128)(2,1)} %collective-permute-done.3), channel_id=1, source_target_pairs={{0,4},{4,0},{8,12},{12,8},{1,5},{5,1},{9,13},{13,9},{2,6},{6,2},{1... | collective-permute-start | bytes 1572872 | tf_op jit(solution)/shard_map/ppermute | solution.py:363
  56.6 46.6 %collective-permute-start.5 = (bf16[256,1024]{1,0:T(8,128)(2,1)}, bf16[256,1024]{1,0:T(8,128)(2,1)S(1)}, u32[]{:S(2)}, u32[]{:S(2)}) collective-permute-start(bf16[256,1024]{1,0:T(8,128)(2,1)} %collective-permute-done.3), channel_id=1, source_target_pairs={{0,8},{4,12},{8,0},{12,4},{1,9},{5,13},{9,1},{13,5},{2,10},{6,14},... | collective-permute-start | bytes 1572872 | tf_op jit(solution)/shard_map/ppermute | solution.py:363
  83.4 19.9 %collective-permute-start.6 = (bf16[256,1024]{1,0:T(8,128)(2,1)}, bf16[256,1024]{1,0:T(8,128)(2,1)S(1)}, u32[]{:S(2)}, u32[]{:S(2)}) collective-permute-start(bf16[256,1024]{1,0:T(8,128)(2,1)} %collective-permute-done.3), channel_id=1, source_target_pairs={{0,12},{4,8},{8,4},{12,0},{1,13},{5,9},{9,5},{13,1},{2,14},{6,10},... | collective-permute-start | bytes 1572872 | tf_op jit(solution)/shard_map/ppermute | solution.py:363
  89.5 96.3 %collective-permute-start.17 = (bf16[4,2,256,1024]{3,2,1,0:T(8,128)(2,1)}, bf16[4,2,256,1024]{3,2,1,0:T(8,128)(2,1)}, u32[]{:S(2)}, u32[]{:S(2)}) collective-permute-start(bf16[4,2,256,1024]{3,2,1,0:T(8,128)(2,1)} %bitcast_dynamic-update-slice_fusion.refs_5_.refs_13_), channel_id=1, source_target_pairs={{0,1},{1,0},{2,3},{3,2},{4,5},{5,4},{6,7},{7,6},{8,9},{9,8},{10,11... | collective-permute-start | bytes 12582920 | tf_op jit(solution)/shard_map/ppermute | solution.py:23
  89.8 13.5 %copy-start.6 = (bf16[1024,1024]{1,0:T(8,128)(2,1)}, bf16[1024,1024]{1,0:T(8,128)(2,1)S(1)}, u32[]{:S(2)}) copy-start(bf16[1024,1024]{1,0:T(8,128)(2,1)S(1)} %pad_maximum_fusion.1.w0_ref) | copy-start | bytes 6291460
  90.1 13.9 %copy-start = (bf16[24,64,1024]{2,1,0:T(8,128)(2,1)S(1)}, bf16[24,64,1024]{2,1,0:T(8,128)(2,1)}, u32[]{:S(2)}) copy-start(bf16[24,64,1024]{2,1,0:T(8,128)(2,1)} %param.29) | copy-start | bytes 9437188
  91.9 20.4 %collective-permute-start.1 = (bf16[8,64,768]{2,1,0:T(8,128)(2,1)S(1)}, bf16[8,64,768]{2,1,0:T(8,128)(2,1)S(1)}, u32[]{:S(2)}, u32[]{:S(2)}) collective-permute-start(bf16[8,64,768]{2,1,0:T(8,128)(2,1)S(1)} %copy-done.10), channel_id=1, source_target_pairs={{0,2},{1,3},{2,0},{3,1},{4,6},{5,7},{6,4},{7,5},{8,10},{9,11},{10,... | collective-permute-start | bytes 2359304 | tf_op jit(solution)/shard_map/ppermute | solution.py:19
  103.2 28.1 %collective-permute-start.7 = (bf16[1024,1024]{1,0:T(8,128)(2,1)S(1)}, bf16[1024,1024]{1,0:T(8,128)(2,1)S(1)}, u32[]{:S(2)}, u32[]{:S(2)}) collective-permute-start(bf16[1024,1024]{1,0:T(8,128)(2,1)S(1)} %pad_maximum_fusion.1.w0_ref), channel_id=1, source_target_pairs={{0,1},{1,0},{2,3},{3,2},{4,5},{5,4},{6,7},{7,6},{8,9},{9,8},{10,11... | collective-permute-start | bytes 6291464 | tf_op jit(solution)/shard_map/ppermute | solution.py:23
  103.4 26.1 %copy-start.27 = (bf16[1024]{0:T(1024)(128)(2,1)S(1)}, bf16[1024]{0:T(1024)(128)(2,1)}, u32[]{:S(2)}) copy-start(bf16[1024]{0:T(1024)(128)(2,1)} %param.17) | copy-start | bytes 6148
  103.4 26.7 %copy-start.28 = (bf16[1024]{0:T(1024)(128)(2,1)S(1)}, bf16[1024]{0:T(1024)(128)(2,1)}, u32[]{:S(2)}) copy-start(bf16[1024]{0:T(1024)(128)(2,1)} %param.24) | copy-start | bytes 6148
  103.4 27.3 %copy-start.29 = (bf16[1024]{0:T(1024)(128)(2,1)S(1)}, bf16[1024]{0:T(1024)(128)(2,1)}, u32[]{:S(2)}) copy-start(bf16[1024]{0:T(1024)(128)(2,1)} %param.28) | copy-start | bytes 6148
  103.4 28.4 %collective-permute-start.8 = (bf16[1024,1024]{1,0:T(8,128)(2,1)S(1)}, bf16[1024,1024]{1,0:T(8,128)(2,1)S(1)}, u32[]{:S(2)}, u32[]{:S(2)}) collective-permute-start(bf16[1024,1024]{1,0:T(8,128)(2,1)S(1)} %constant_dynamic-update-slice_fusion.w1_ref), channel_id=1, source_target_pairs={{0,1},{1,0},{2,3},{3,2},{4,5},{5,4},{6,7},{7,6},{8,9},{9,8},{10,11... | collective-permute-start | bytes 6291464 | tf_op jit(solution)/shard_map/ppermute | solution.py:23
  105.5 26.3 %copy-start.11 = (bf16[6,64,1024]{2,1,0:T(8,128)(2,1)}, bf16[6,64,1024]{2,1,0:T(8,128)(2,1)S(1)}, u32[]{:S(2)}) copy-start(bf16[6,64,1024]{2,1,0:T(8,128)(2,1)S(1)} %get-tuple-element.105) | copy-start | bytes 2359300
  105.5 22.8 %collective-permute-start.2 = (bf16[8,64,768]{2,1,0:T(8,128)(2,1)S(1)}, bf16[8,64,768]{2,1,0:T(8,128)(2,1)S(1)}, u32[]{:S(2)}, u32[]{:S(2)}) collective-permute-start(bf16[8,64,768]{2,1,0:T(8,128)(2,1)S(1)} %copy-done.9), channel_id=1, source_target_pairs={{0,3},{1,2},{2,1},{3,0},{4,7},{5,6},{6,5},{7,4},{8,11},{9,10},{10,... | collective-permute-start | bytes 2359304 | tf_op jit(solution)/shard_map/ppermute | solution.py:90
  112.4 20.6 %copy-start.32 = (bf16[8,64,768]{2,1,0:T(8,128)(2,1)}, bf16[8,64,768]{2,1,0:T(8,128)(2,1)S(1)}, u32[]{:S(2)}) copy-start(bf16[8,64,768]{2,1,0:T(8,128)(2,1)S(1)} %collective-permute-done.1.p2_ref.e2_ref.refs_9_) | copy-start | bytes 2359300
  112.4 16.2 %collective-permute-start.9 = (bf16[6,64,1024]{2,1,0:T(8,128)(2,1)S(1)}, bf16[6,64,1024]{2,1,0:T(8,128)(2,1)S(1)}, u32[]{:S(2)}, u32[]{:S(2)}) collective-permute-start(bf16[6,64,1024]{2,1,0:T(8,128)(2,1)S(1)} %get-tuple-element.105), channel_id=1, source_target_pairs={{0,1},{1,0},{2,3},{3,2},{4,5},{5,4},{6,7},{7,6},{8,9},{9,8},{10,11... | collective-permute-start | bytes 2359304 | tf_op jit(solution)/shard_map/ppermute | solution.py:23
  128.3 57.5 %collective-permute-start.16 = (bf16[1024,1024]{1,0:T(8,128)(2,1)}, bf16[1024,1024]{1,0:T(8,128)(2,1)}, u32[]{:S(2)}, u32[]{:S(2)}) collective-permute-start(bf16[1024,1024]{1,0:T(8,128)(2,1)} %w1_ref.1), channel_id=1, source_target_pairs={{0,1},{1,0},{2,3},{3,2},{4,5},{5,4},{6,7},{7,6},{8,9},{9,8},{10,11... | collective-permute-start | bytes 6291464 | tf_op jit(solution)/shard_map/ppermute | solution.py:23
  129.2 3.8 copy-start.34
  129.2 56.6 %collective-permute-start.18 = (bf16[1024,1024]{1,0:T(8,128)(2,1)}, bf16[1024,1024]{1,0:T(8,128)(2,1)}, u32[]{:S(2)}, u32[]{:S(2)}) collective-permute-start(bf16[1024,1024]{1,0:T(8,128)(2,1)} %w2_ref.1), channel_id=1, source_target_pairs={{0,1},{1,0},{2,3},{3,2},{4,5},{5,4},{6,7},{7,6},{8,9},{9,8},{10,11... | collective-permute-start | bytes 6291464 | tf_op jit(solution)/shard_map/ppermute | solution.py:23
  131.3 54.2 %collective-permute-start.10 = (bf16[6,64,1024]{2,1,0:T(8,128)(2,1)}, bf16[6,64,1024]{2,1,0:T(8,128)(2,1)}, u32[]{:S(2)}, u32[]{:S(2)}) collective-permute-start(bf16[6,64,1024]{2,1,0:T(8,128)(2,1)} %get-tuple-element.77), channel_id=1, source_target_pairs={{0,2},{1,3},{2,0},{3,1},{4,6},{5,7},{6,4},{7,5},{8,10},{9,11},{10,... | collective-permute-start | bytes 2359304 | tf_op jit(solution)/shard_map/ppermute | solution.py:19
  132.7 53.2 %collective-permute-start.11 = (bf16[6,64,1024]{2,1,0:T(8,128)(2,1)}, bf16[6,64,1024]{2,1,0:T(8,128)(2,1)}, u32[]{:S(2)}, u32[]{:S(2)}) collective-permute-start(bf16[6,64,1024]{2,1,0:T(8,128)(2,1)} %get-tuple-element.103), channel_id=1, source_target_pairs={{0,3},{1,2},{2,1},{3,0},{4,7},{5,6},{6,5},{7,4},{8,11},{9,10},{10,... | collective-permute-start | bytes 2359304 | tf_op jit(solution)/shard_map/ppermute | solution.py:90
  185.6 284.1 %collective-permute-start.22 = (bf16[1536,2560]{1,0:T(8,128)(2,1)}, bf16[1536,2560]{1,0:T(8,128)(2,1)}, u32[]{:S(2)}, u32[]{:S(2)}) collective-permute-start(bf16[1536,2560]{1,0:T(8,128)(2,1)} %get-tuple-element.51.la_ref), channel_id=1, source_target_pairs={{0,1},{1,0},{2,3},{3,2},{4,5},{5,4},{6,7},{7,6},{8,9},{9,8},{10,11... | collective-permute-start | bytes 23592968 | tf_op jit(solution)/shard_map/ppermute | solution.py:23
  324.4 149.1 %collective-permute-start.23 = (bf16[1536,1536]{1,0:T(8,128)(2,1)}, bf16[1536,1536]{1,0:T(8,128)(2,1)}, u32[]{:S(2)}, u32[]{:S(2)}) collective-permute-start(bf16[1536,1536]{1,0:T(8,128)(2,1)} %get-tuple-element.56), channel_id=1, source_target_pairs={{0,1},{1,0},{2,3},{3,2},{4,5},{5,4},{6,7},{7,6},{8,9},{9,8},{10,11... | collective-permute-start | bytes 14155784 | tf_op jit(solution)/shard_map/ppermute | solution.py:23
  324.7 294.0 %collective-permute-start.32 = (bf16[1536,3072]{1,0:T(8,128)(2,1)}, bf16[1536,3072]{1,0:T(8,128)(2,1)}, u32[]{:S(2)}, u32[]{:S(2)}) collective-permute-start(bf16[1536,3072]{1,0:T(8,128)(2,1)} %get-tuple-element.74.da_ref), channel_id=1, source_target_pairs={{0,1},{1,0},{2,3},{3,2},{4,5},{5,4},{6,7},{7,6},{8,9},{9,8},{10,11... | collective-permute-start | bytes 28311560 | tf_op jit(solution)/shard_map/ppermute | solution.py:23
  324.9 20.0 %collective-permute-start.34 = (bf16[6,64,1024]{2,1,0:T(8,128)(2,1)}, bf16[6,64,1024]{2,1,0:T(8,128)(2,1)}, u32[]{:S(2)}, u32[]{:S(2)}) collective-permute-start(bf16[6,64,1024]{2,1,0:T(8,128)(2,1)} %get-tuple-element.106.refs_0_), channel_id=1, source_target_pairs={{0,2},{1,3},{2,0},{3,1},{4,6},{5,7},{6,4},{7,5},{8,10},{9,11},{10,... | collective-permute-start | bytes 2359304 | tf_op jit(solution)/shard_map/ppermute | solution.py:19
  326.2 18.7 %copy-start.12 = (bf16[6,64,1024]{2,1,0:T(8,128)(2,1)S(1)}, bf16[6,64,1024]{2,1,0:T(8,128)(2,1)}, u32[]{:S(2)}) copy-start(bf16[6,64,1024]{2,1,0:T(8,128)(2,1)} %copy-done.11) | copy-start | bytes 2359300
  327.8 37.0 %collective-permute-start.24 = (f32[384,1024]{1,0:T(8,128)S(1)}, f32[384,1024]{1,0:T(8,128)}, u32[]{:S(2)}, u32[]{:S(2)}) collective-permute-start(f32[384,1024]{1,0:T(8,128)S(1)} %constant_dynamic-slice_fusion), channel_id=1, source_target_pairs={{0,1},{1,0},{2,3},{3,2},{4,5},{5,4},{6,7},{7,6},{8,9},{9,8},{10,11... | collective-permute-start | bytes 4718600 | tf_op jit(solution)/shard_map/ppermute | solution.py:23
  344.9 19.8 %collective-permute-start.35 = (bf16[6,64,1024]{2,1,0:T(8,128)(2,1)S(1)}, bf16[6,64,1024]{2,1,0:T(8,128)(2,1)S(1)}, u32[]{:S(2)}, u32[]{:S(2)}) collective-permute-start(bf16[6,64,1024]{2,1,0:T(8,128)(2,1)S(1)} %copy-done.12), channel_id=1, source_target_pairs={{0,3},{1,2},{2,1},{3,0},{4,7},{5,6},{6,5},{7,4},{8,11},{9,10},{10,... | collective-permute-start | bytes 2359304 | tf_op jit(solution)/shard_map/ppermute | solution.py:90
  364.7 4.2 collective-permute-start.36
  365.6 118.7 %collective-permute-start.33 = (bf16[1536,1024]{1,0:T(8,128)(2,1)}, bf16[1536,1024]{1,0:T(8,128)(2,1)}, u32[]{:S(2)}, u32[]{:S(2)}) collective-permute-start(bf16[1536,1024]{1,0:T(8,128)(2,1)} %get-tuple-element.48.h_ref.ha_ref), channel_id=1, source_target_pairs={{0,2},{1,3},{2,0},{3,1},{4,6},{5,7},{6,4},{7,5},{8,10},{9,11},{10,... | collective-permute-start | bytes 9437192 | tf_op jit(solution)/shard_map/ppermute | solution.py:19
  368.9 100.7 %collective-permute-start.25 = (f32[384,1024]{1,0:T(8,128)S(1)}, f32[384,1024]{1,0:T(8,128)S(1)}, u32[]{:S(2)}, u32[]{:S(2)}) collective-permute-start(f32[384,1024]{1,0:T(8,128)S(1)} %dynamic-slice_add_fusion), channel_id=1, source_target_pairs={{0,2},{1,3},{2,0},{3,1},{4,6},{5,7},{6,4},{7,5},{8,10},{9,11},{10,... | collective-permute-start | bytes 4718600 | tf_op jit(solution)/shard_map/ppermute | solution.py:19
  469.6 57.5 %collective-permute-start.30 = (bf16[1536,1024]{1,0:T(8,128)(2,1)}, bf16[1536,1024]{1,0:T(8,128)(2,1)}, u32[]{:S(2)}, u32[]{:S(2)}) collective-permute-start(bf16[1536,1024]{1,0:T(8,128)(2,1)} %get-tuple-element.53.dx_ref.la_ref), channel_id=1, source_target_pairs={{0,1},{1,0},{2,3},{3,2},{4,5},{5,4},{6,7},{7,6},{8,9},{9,8},{10,11... | collective-permute-start | bytes 9437192 | tf_op jit(solution)/shard_map/ppermute | solution.py:23
  469.6 15.2 %collective-permute-start.19 = (bf16[6,64,1024]{2,1,0:T(8,128)(2,1)}, bf16[6,64,1024]{2,1,0:T(8,128)(2,1)}, u32[]{:S(2)}, u32[]{:S(2)}) collective-permute-start(bf16[6,64,1024]{2,1,0:T(8,128)(2,1)} %get-tuple-element.101), channel_id=1, source_target_pairs={{0,1},{1,0},{2,3},{3,2},{4,5},{5,4},{6,7},{7,6},{8,9},{9,8},{10,11... | collective-permute-start | bytes 2359304 | tf_op jit(solution)/shard_map/ppermute | solution.py:23
  472.3 15.1 %copy-start.16 = (f32[1,1024]{1,0:T(1,128)}, f32[1,1024]{1,0:T(1,128)S(1)}, u32[]{:S(2)}) copy-start(f32[1,1024]{1,0:T(1,128)S(1)} %slice.118) | copy-start | bytes 12292
  473.5 20.8 %collective-permute-start.20 = (bf16[6,64,1024]{2,1,0:T(8,128)(2,1)}, bf16[6,64,1024]{2,1,0:T(8,128)(2,1)}, u32[]{:S(2)}, u32[]{:S(2)}) collective-permute-start(bf16[6,64,1024]{2,1,0:T(8,128)(2,1)} %get-tuple-element.100), channel_id=1, source_target_pairs={{0,2},{1,3},{2,0},{3,1},{4,6},{5,7},{6,4},{7,5},{8,10},{9,11},{10,... | collective-permute-start | bytes 2359304 | tf_op jit(solution)/shard_map/ppermute | solution.py:19
  474.4 11.3 %copy-start.23 = (f32[1,3072]{1,0:T(1,128)S(1)}, f32[1,3072]{1,0:T(1,128)}, u32[]{:S(2)}) copy-start(f32[1,3072]{1,0:T(1,128)} %get-tuple-element.68) | copy-start | bytes 36868
  474.4 11.3 %copy-start.2 = (f32[256,1024]{1,0:T(8,128)S(1)}, f32[256,1024]{1,0:T(8,128)}, u32[]{:S(2)}) copy-start(f32[256,1024]{1,0:T(8,128)} %get-tuple-element.65) | copy-start | bytes 3145732
  484.3 25.1 %collective-permute-start.21 = (bf16[6,64,1024]{2,1,0:T(8,128)(2,1)}, bf16[6,64,1024]{2,1,0:T(8,128)(2,1)}, u32[]{:S(2)}, u32[]{:S(2)}) collective-permute-start(bf16[6,64,1024]{2,1,0:T(8,128)(2,1)} %get-tuple-element.99), channel_id=1, source_target_pairs={{0,3},{1,2},{2,1},{3,0},{4,7},{5,6},{6,5},{7,4},{8,11},{9,10},{10,... | collective-permute-start | bytes 2359304 | tf_op jit(solution)/shard_map/ppermute | solution.py:90
  484.8 10.0 %collective-permute-start.26 = (bf16[384,1024]{1,0:T(8,128)(2,1)S(1)}, bf16[384,1024]{1,0:T(8,128)(2,1)}, u32[]{:S(2)}, u32[]{:S(2)}) collective-permute-start(bf16[384,1024]{1,0:T(8,128)(2,1)S(1)} %add_convert_fusion.1), channel_id=1, source_target_pairs={{0,1},{1,0},{2,3},{3,2},{4,5},{5,4},{6,7},{7,6},{8,9},{9,8},{10,11... | collective-permute-start | bytes 2359304 | tf_op jit(solution)/shard_map/ppermute | solution.py:23
  486.6 12.3 %copy-start.18 = (f32[1,1024]{1,0:T(1,128)}, f32[1,1024]{1,0:T(1,128)S(1)}, u32[]{:S(2)}) copy-start(f32[1,1024]{1,0:T(1,128)S(1)} %get-tuple-element.123) | copy-start | bytes 12292
  486.6 12.3 %copy-start.20 = (f32[1,1024]{1,0:T(1,128)}, f32[1,1024]{1,0:T(1,128)S(1)}, u32[]{:S(2)}) copy-start(f32[1,1024]{1,0:T(1,128)S(1)} %get-tuple-element.124) | copy-start | bytes 12292
  487.4 23.5 %copy-start.8 = (bf16[6,64,1024]{2,1,0:T(8,128)(2,1)S(1)}, bf16[6,64,1024]{2,1,0:T(8,128)(2,1)}, u32[]{:S(2)}) copy-start(bf16[6,64,1024]{2,1,0:T(8,128)(2,1)} %copy-done.7) | copy-start | bytes 2359300
  494.2 19.8 %collective-permute-start.27 = (f32[138,1024]{1,0:T(8,128)}, f32[138,1024]{1,0:T(8,128)}, u32[]{:S(2)}, u32[]{:S(2)}) collective-permute-start(f32[138,1024]{1,0:T(8,128)} %concatenate.87), channel_id=1, source_target_pairs={{0,1},{1,0},{2,3},{3,2},{4,5},{5,4},{6,7},{7,6},{8,9},{9,8},{10,11... | collective-permute-start | bytes 1695752 | tf_op jit(solution)/shard_map/ppermute | solution.py:23
  494.8 117.9 %collective-permute-start.29 = (f32[1024,768]{1,0:T(8,128)}, f32[1024,768]{1,0:T(8,128)}, u32[]{:S(2)}, u32[]{:S(2)}) collective-permute-start(f32[1024,768]{1,0:T(8,128)} %shard_map.257), channel_id=1, source_target_pairs={{0,2},{1,3},{2,0},{3,1},{4,6},{5,7},{6,4},{7,5},{8,10},{9,11},{10,... | collective-permute-start | bytes 9437192 | tf_op jit(solution)/shard_map/ppermute | solution.py:19
  509.5 109.2 %collective-permute-start.37 = (bf16[1536,1024]{1,0:T(8,128)(2,1)}, bf16[1536,1024]{1,0:T(8,128)(2,1)}, u32[]{:S(2)}, u32[]{:S(2)}) collective-permute-start(bf16[1536,1024]{1,0:T(8,128)(2,1)} %collective-permute-done.33.hx_ref), channel_id=1, source_target_pairs={{0,1},{1,0},{2,3},{3,2},{4,5},{5,4},{6,7},{7,6},{8,9},{9,8},{10,11... | collective-permute-start | bytes 9437192 | tf_op jit(solution)/shard_map/ppermute | solution.py:23
  510.9 3.2 copy-start.21
  510.9 3.2 copy-start.22
  514.0 104.7 %collective-permute-start.38 = (bf16[1536,1024]{1,0:T(8,128)(2,1)}, bf16[1536,1024]{1,0:T(8,128)(2,1)}, u32[]{:S(2)}, u32[]{:S(2)}) collective-permute-start(bf16[1536,1024]{1,0:T(8,128)(2,1)} %bitcast.23.dx_ref), channel_id=1, source_target_pairs={{0,1},{1,0},{2,3},{3,2},{4,5},{5,4},{6,7},{7,6},{8,9},{9,8},{10,11... | collective-permute-start | bytes 9437192 | tf_op jit(solution)/shard_map/ppermute | solution.py:23
  527.0 61.1 %copy-start.4 = (f32[138,1024]{1,0:T(8,128)}, f32[138,1024]{1,0:T(8,128)S(1)}, u32[]{:S(2)}) copy-start(f32[138,1024]{1,0:T(8,128)S(1)} %add.146) | copy-start | bytes 1695748
  527.1 56.6 %collective-permute-start.28 = (f32[72,1024]{1,0:T(8,128)S(1)}, f32[72,1024]{1,0:T(8,128)S(1)}, u32[]{:S(2)}, u32[]{:S(2)}) collective-permute-start(f32[72,1024]{1,0:T(8,128)S(1)} %pad_maximum_fusion.11), channel_id=1, source_target_pairs={{0,2},{1,3},{2,0},{3,1},{4,6},{5,7},{6,4},{7,5},{8,10},{9,11},{10,... | collective-permute-start | bytes 884744 | tf_op jit(solution)/shard_map/ppermute | solution.py:19
  583.7 4.4 copy-start.14
  583.8 24.5 %collective-permute-start.31 = (f32[1024,256]{1,0:T(8,128)}, f32[1024,256]{1,0:T(8,128)}, u32[]{:S(2)}, u32[]{:S(2)}) collective-permute-start(f32[1024,256]{1,0:T(8,128)} %get-tuple-element.72), channel_id=1, source_target_pairs={{0,2},{1,3},{2,0},{3,1},{4,6},{5,7},{6,4},{7,5},{8,10},{9,11},{10,... | collective-permute-start | bytes 3145736 | tf_op jit(solution)/shard_map/ppermute | solution.py:19
  588.2 24.5 %copy-start.1 = (f32[1024,768]{1,0:T(8,128)S(1)}, f32[1024,768]{1,0:T(8,128)}, u32[]{:S(2)}) copy-start(f32[1024,768]{1,0:T(8,128)} %shard_map.258) | copy-start | bytes 9437188
  (11 other events, 22.4 us)

commit v2 on v1

--- a/solution.py
+++ b/solution.py
@@ -12,7 +12,6 @@
 LANES = 128
 GELU_A = 0.7978845608028654
 GELU_B = 0.044715
-MLP_TILE = 256
 
 
 def x_swap(val):
@@ -225,25 +224,6 @@
                16 * rows * dim * dim, [pltpu.VMEM((tile, dim), WIDE)])(qkv, d_x, emb, *got, scale, *weights)
 
 
-def weight_spec(weight):
-    val, at = weight
-    if val.ndim == 2:
-        return held(val.shape)
-    return pl.BlockSpec((val.shape[0], 1) + val.shape[2:], lambda i: (0, at, 0, 0), pipeline_mode=pl.Buffered(1))
-
-
-def w_cols(ref, cols):
-    if len(ref.shape) == 2:
-        return ref[:, cols]
-    return ref[:, 0, :, cols].reshape(ref.shape[0] * ref.shape[2], STEP)
-
-
-def w_rows(ref, rows):
-    if len(ref.shape) == 2:
-        return ref[rows, :]
-    return ref[rows.start // STEP, 0]
-
-
 def gelu_both(pre, d_hidden):
     d_hidden = d_hidden.astype(HALF).astype(WIDE)
     square = pre * pre
@@ -253,46 +233,75 @@
     return (pre * cdf).astype(HALF), d_hidden * slope
 
 
-def up(h_val, d_val, w1_ref, bias, w2_ref, store):
+def up(h_val, d_val, w1_cols, bias, w2_rows, store):
     waiting = None
     for cols in chunks(bias.shape[1]):
-        ready = (cols, mm(h_val, w_cols(w1_ref, cols)), mm_nt(d_val, w_rows(w2_ref, cols)))
+        ready = (cols, mm(h_val, w1_cols(cols)), mm_nt(d_val, w2_rows(cols)))
         if waiting is not None:
             store(waiting[0], *gelu_both(waiting[1] + bias[:, waiting[0]], waiting[2]))
         waiting = ready
     store(waiting[0], *gelu_both(waiting[1] + bias[:, waiting[0]], waiting[2]))
 
 
-def mlp_kernel(h_ref, x_ref, b2_ref, scale_ref, *refs):
-    d_refs, w1_refs, b1_refs, w2_refs = refs[:4], refs[4:8], refs[8:12], refs[12:16]
-    own_ref, pack_ref, out_ref, dx_ref, sum_ref, bsum_ref, g_ref, p_ref, acc_ref, dacc_ref = refs[16:]
+def mlp_kernel(h_ref, x_ref, b2_ref, scale_ref, d0_ref, d1_ref, d2_ref, d3_ref, *refs):
+    b_refs, near_refs, x_refs, diag_refs = [refs[i:i + 4] for i in range(0, 16, 4)]
+    o0_ref, o1_ref, o2_ref, o3_ref, own_ref, pack_ref, dx_ref, sum_ref, bsum_ref, g_ref, p_ref, acc_ref, dacc_ref, w_ref, sem = refs[16:]
     first_step(sum_ref, bsum_ref)
     dim = h_ref.shape[1]
     cols_n = g_ref.shape[1]
-    d_two = rows_of(d_refs)
+    group = lax.axis_index('dp')
+    spots = (group, group + 1 - 2 * (group % 2), (group + 2) % 4, 3 - group)
+
+    def copies(side):
+        if side % 2:
+            moves = [(ref, w_ref.at[side, at]) for ref, at in zip(diag_refs if side > 1 else x_refs, spots)]
+        else:
+            moves = [(near_refs[side + which], w_ref.at[side, :, which]) for which in range(2)]
+        return [pltpu.make_async_copy(*move, sem.at[side, k]) for k, move in enumerate(moves)]
+
+    @pl.when(pl.program_id(0) == 0)
+    def _():
+        pending = [copy for side in range(4) for copy in copies(side)]
+        for copy in pending:
+            copy.start()
+        for copy in pending:
+            copy.wait()
+
+    d_two = rows_of((d0_ref, d1_ref, d2_ref, d3_ref))
     pack_ref[:, 2 * dim:] = d_two
     for side in range(4):
+        def w1_cols(cols):
+            return w_ref[side, :, 0, :, cols].reshape(dim, STEP)
+
+        def w2_cols(cols):
+            return w_ref[side, :, 1, :, cols].reshape(cols_n, STEP)
+
+        def w1_rows(rows):
+            return w_ref[side, rows.start // STEP, 0]
+
+        def w2_rows(rows):
+            return w_ref[side, rows.start // STEP, 1]
+
         def store(cols, hidden, d_pre):
             d_pre_h = d_pre.astype(HALF)
             g_ref[:, cols] = hidden
             p_ref[:, cols] = d_pre_h
-            shifted = slice(cols_n + cols.start, cols_n + cols.stop)
-            if side == 0:
-                own_ref[:, cols] = hidden
-                own_ref[:, shifted] = d_pre_h
-            if side == 2:
-                pack_ref[:, cols] = hidden
-                pack_ref[:, shifted] = d_pre_h
-            if side in (0, 2):
+            if side % 2 == 0:
+                to_ref = pack_ref if side else own_ref
+                to_ref[:, cols] = hidden
+                to_ref[:, cols_n + cols.start:cols_n + cols.stop] = d_pre_h
                 bsum_ref[side // 2:side // 2 + 1, cols] += jnp.sum(d_pre, axis=0, keepdims=True)
 
-        up(h_ref[...], d_two, w1_refs[side], row_of(b1_refs[side], 2, cols_n), w2_refs[side], store)
+        up(h_ref[...], d_two, w1_cols, row_of(b_refs[side], 2, cols_n), w2_rows, store)
         for cols in chunks(dim):
-            total = mm(g_ref[...], w_cols(w2_refs[side], cols))
-            d_total = mm_nt(p_ref[...], w_rows(w1_refs[side], cols))
-            acc_ref[:, cols] = total if side == 0 else acc_ref[:, cols] + total
-            dacc_ref[:, cols] = d_total if side == 0 else dacc_ref[:, cols] + d_total
-    out_ref[...] = (x_ref[...].astype(WIDE) + (acc_ref[...] + b2_ref[...].astype(WIDE))).astype(HALF)
+            total = mm(g_ref[...], w2_cols(cols))
+            d_total = mm_nt(p_ref[...], w1_rows(cols))
+            acc_ref[:, cols] = acc_ref[:, cols] + total if side else total
+            dacc_ref[:, cols] = dacc_ref[:, cols] + d_total if side else d_total
+    x_two = (x_ref[...].astype(WIDE) + (acc_ref[...] + b2_ref[...].astype(WIDE))).astype(HALF)
+    for k, ref in enumerate((o0_ref, o1_ref, o2_ref, o3_ref)):
+        n_tok = ref.shape[1]
+        ref[0] = x_two[k * n_tok:(k + 1) * n_tok]
     d_h = dacc_ref[...].astype(HALF).astype(WIDE)
     d_ln, d_scale, d_bias = normalize_back(x_ref[...].astype(WIDE), scale_ref[1:2, :].astype(WIDE), d_h)
     d_x = (pack_ref[:, 2 * dim:].astype(WIDE) + d_ln).astype(HALF)
@@ -300,13 +309,14 @@
     sum_ref[...] += jnp.concatenate([d_scale, d_bias, jnp.sum(d_x.astype(WIDE), axis=0, keepdims=True), jnp.zeros((5, dim), WIDE)], axis=0)
 
 
-def mlp(h_val, d_blocks, x_val, b2, scale, w1s, biases, w2s):
-    rows, dim, cols, tile = h_val.shape[0], h_val.shape[1], w2s[0][0].shape[0], MLP_TILE
-    specs = [tiled(tile, dim)] * 2 + [held(b2.shape), held(scale.shape)] + image_blocks(d_blocks, tile * d_blocks[0].shape[0] // rows) + [weight_spec(w) for w in w1s] + extra_blocks(biases) + [weight_spec(w) for w in w2s]
-    outs = [shape_of(rows, 2 * cols), shape_of(rows, 3 * dim), shape_of(rows, dim), shape_of(rows, dim), shape_of(8, dim, dtype=WIDE), shape_of(8, cols, dtype=WIDE)]
-    scratch = [pltpu.VMEM((tile, cols), HALF)] * 2 + [pltpu.VMEM((tile, dim), WIDE)] * 2
-    return run(mlp_kernel, rows // tile, specs, [tiled(tile, o.shape[1]) for o in outs[:4]] + [fixed(o.shape) for o in outs[4:]], outs,
-               32 * rows * dim * cols, scratch)(h_val, x_val, b2, scale, *d_blocks, *[w[0] for w in w1s], *biases, *[w[0] for w in w2s])
+def mlp(h_val, d_blocks, x_val, b2, scale, biases, near_ws, x_ws, diag_ws):
+    (rows, dim), cols, tile = h_val.shape, near_ws[0].shape[2], 256
+    far = [*near_ws, *x_ws, *diag_ws]
+    specs = [tiled(tile, dim)] * 2 + [held(b2.shape), held(scale.shape)] + image_blocks(d_blocks) + extra_blocks(biases) + [pl.BlockSpec(memory_space=pl.ANY)] * len(far)
+    outs = [shape_of(*val.shape) for val in d_blocks] + [shape_of(rows, width) for width in (2 * cols, 3 * dim, dim)] + [shape_of(8, width, dtype=WIDE) for width in (dim, cols)]
+    scratch = [pltpu.VMEM((tile, cols), HALF)] * 2 + [pltpu.VMEM((tile, dim), WIDE)] * 2 + [pltpu.VMEM((4, 4) + x_ws[0].shape, HALF), pltpu.SemaphoreType.DMA((4, 4))]
+    return run(mlp_kernel, rows // tile, specs, image_blocks(d_blocks) + [tiled(tile, o.shape[1]) for o in outs[4:7]] + [fixed(o.shape) for o in outs[7:]], outs,
+               32 * rows * dim * cols, scratch)(h_val, x_val, b2, scale, *d_blocks, *biases, *far)
 
 
 def grad_kernel(la_ref, lb_ref, ra_ref, rb_ref, *out_refs):
@@ -336,7 +346,7 @@
             p_ref[at, :, cols] = d_pre.astype(HALF)
             bsum_ref[:, cols] += jnp.sum(d_pre, axis=0, keepdims=True)
 
-        up(h_ref[...], d_ref[...], w1_ref, b1_ref[...].astype(WIDE), w2_ref, store)
+        up(h_ref[...], d_ref[...], lambda cols: w1_ref[:, cols], b1_ref[...].astype(WIDE), lambda cols: w2_ref[cols, :], store)
     for rows in chunks(acc1_ref.shape[0]):
         acc1_ref[rows, :] += mm_tn(ha_ref[:, rows], ga_ref[:, cols_n:]) + mm_tn(hb_ref[:, rows], gb_ref[:, cols_n:]) + mm_tn(hx_ref[:, rows], p_ref[0]) + mm_tn(hd_ref[:, rows], p_ref[1])
     for rows in chunks(acc2_ref.shape[0]):
@@ -405,10 +415,9 @@
     for val, at in attn_pieces:
         attn_x = lax.dynamic_update_slice(attn_x, val, (at * (dim // 4), 0))
     attn_d = core_swap(attn_x)
-    mlp_x = jnp.zeros((4, 2, dim // 4, cols), HALF)
-    for val, at in mlp_pieces:
-        mlp_x = lax.dynamic_update_slice(mlp_x, val[None], (at, 0, 0, 0))
-    mlp_d = core_swap(mlp_x)
+    mlp_x = [val for val, _ in mlp_pieces]
+    mlp_d = [core_swap(val) for val in mlp_x]
+    mlp_near = [val.reshape(4, dim // 4, cols) for val in (fc1_w, fc2_w, fc1_c, fc2_c)]
     attn_ws = (attn_w, attn_x, attn_c, attn_d)
 
     emb, qkv, ctx, x_one, h_two, pack_f = front(got, patch_w, row(patch_b), ln_scale, ln_bias, row(out_b), attn_ws)
@@ -416,11 +425,9 @@
     pack_f_c = core_swap(pack_f)
     h_two_d = core_swap(h_two_x)
 
-    w1s, w2s = ((fc1_w, 0), (mlp_x, 0), (fc1_c, 0), (mlp_d, 0)), ((fc2_w, 0), (mlp_x, 1), (fc2_c, 0), (mlp_d, 1))
-    own_gp, pack_m, x_two, d_x, sums_two, b_sums = mlp(h_two, d_blocks, x_one, row(fc2_b), ln_scale, w1s, (got[0], got[2], got[1], got[3]), w2s)
+    *x_blocks, own_gp, pack_m, d_x, sums_two, b_sums = mlp(h_two, d_blocks, x_one, row(fc2_b), ln_scale, (got[0], got[2], got[1], got[3]), mlp_near, mlp_x, mlp_d)
     pack_m_c = core_swap(pack_m)
-    x_blocks = x_two.reshape(n_own, 4, n_tok, dim)
-    x_parts = (x_blocks[:, 0], core_swap(x_blocks[:, 1]), x_swap(x_blocks[:, 2]), diag_swap(x_blocks[:, 3]))
+    x_parts = (x_blocks[0], core_swap(x_blocks[1]), x_swap(x_blocks[2]), diag_swap(x_blocks[3]))
     d_x_c = core_swap(d_x)
     d_o_own, d_o_x = grad(((d_x, dim, 0), (d_x_c, dim, 0), (ctx, 2 * heads, 0), (pack_f_c, 2 * heads, 4)), 2)
     d_o_recv = x_swap(d_o_x)

time: 680 us -> 719 us (1.057)
  waiting for transfers between devices: 301 us -> 347 us
  local copies, waits for them, and re-layouts: 44.5 us -> 34 us
    ppermute x11, waiting for transfers between devices: 215 us -> 237 us  [x_swap(): return lax.ppermute(val, 'tp', X_PAIRS)]
    ppermute x4, waiting for transfers between devices: 45.8 us -> 60.3 us  [diag_swap(): return lax.ppermute(val, 'tp', DIAG_PAIRS)]
    ppermute x6, waiting for transfers between devices: 40.4 us -> 49.8 us  [gather_pieces(): lax.ppermute(pieces[0][0], 'dp', [(i, i ^ hop) for i in range(4)])]
    dynamic_update_slice x4 -> x0, local copies, waits for them, and re-layouts: 7.93 us -> none  [group_step(): mlp_x = lax.dynamic_update_slice(mlp_x, val[None], (at, 0, 0, 0))]
  transfers between devices with their start and end apart: 39 -> 42, of which waited for: 14 -> 16; matrix products, arithmetic and copies ran while one was open for 10% -> 7% of each run, Pallas kernels for 32% -> 31%
where the time goes in v2:
time: 719 us; the launch traced here: 711 us
  waiting for transfers between devices  347 us (48%)
  Pallas kernels  271 us (38%)
  local copies, waits for them, and re-layouts  34 us (5%)
  other arithmetic  29 us (4%)
  starting transfers between devices  28.9 us (4%)
    ppermute x11, waiting for transfers between devices, x_swap(): return lax.ppermute(val, 'tp', X_PAIRS)  237 us
    pallas_call x1, Pallas kernels, mlp(): run(mlp_kernel, rows // tile, specs, image_blocks(d_blocks) + [tiled(tile...  74.9 us
    pallas_call x1, Pallas kernels, rear(): run(rear_kernel, rows // tile, specs, [tiled(tile, 3 * dim // 2)] * 2 + [...  64.8 us
    ppermute x4, waiting for transfers between devices, diag_swap(): return lax.ppermute(val, 'tp', DIAG_PAIRS)  60.3 us
    pallas_call x1, Pallas kernels, front(): run(front_kernel, n_own, image_blocks(got) + extra_blocks(got) + [held(v....  52.2 us
    pallas_call x1, Pallas kernels, grad_mlp(): run(grad_mlp_kernel, rows // tile, [block(tile, width, at) for _, width,...  51.5 us
    ppermute x6, waiting for transfers between devices, gather_pieces(): lax.ppermute(pieces[0][0], 'dp', [(i, i ^ hop) for i in range(4)])  49.8 us
    pallas_call x3, Pallas kernels, grad(): run(grad_kernel, rows // tile, [block(tile, size, at) for _, size, at in...  27.5 us
  transfers between devices with their start and end apart: 42, of which 16 were waited for; matrix products, arithmetic and copies ran while one was open for 7% of the time, Pallas kernels for 31%

profile of v2, /device:TPU:0, one launch (start us, length us, event | category | flops | bytes accessed | tf_op | source)
XLA Modules:
  0.0 711.1 jit_solution(10768109143883822630)
XLA Ops:
  2.9 0.9 fusion.5
  3.9 1.8 constant_dynamic-slice_fusion.5
  5.7 1.5 pad_maximum_fusion.2
  8.2 1.7 copy.34
  10.0 2.5 collective-permute-start.3
  12.5 1.0 collective-permute-start.1
  14.1 11.2 %collective-permute-done.3 = bf16[256,1024]{1,0:T(8,128)(2,1)S(1)} collective-permute-done((bf16[256,1024]{1,0:T(8,128)(2,1)S(1)}, bf16[256,1024]{1,0:T(8,128)(2,1)S(1)}, u32[]{:S(2)}, u32[]{:S(2)}) %collective-permute-start.3) | collective-permute-done | bytes 524320 | tf_op jit(solution)/shard_map/ppermute | solution.py:18
  25.3 2.0 collective-permute-start.4
  27.3 1.6 collective-permute-start.5
  28.9 1.6 pad_maximum_fusion.1.w0_ref
  30.5 1.5 constant_dynamic-slice_fusion.1
  32.0 10.1 %collective-permute-done.1.p2_ref.e2_ref.refs_1_ = bf16[8,64,768]{2,1,0:T(8,128)(2,1)S(1)} collective-permute-done((bf16[8,64,768]{2,1,0:T(8,128)(2,1)S(1)}, bf16[8,64,768]{2,1,0:T(8,128)(2,1)S(1)}, u32[]{:S(2)}, u32[]{:S(2)}) %collective-permute-start.1) | collective-permute-done | bytes 786464 | tf_op jit(solution)/shard_map/ppermute | solution.py:18
  42.1 1.4 dynamic-slice_bitcast_fusion
  43.5 15.1 %collective-permute-done.2.p3_ref.e3_ref.refs_3_ = bf16[8,64,768]{2,1,0:T(8,128)(2,1)S(1)} collective-permute-done((bf16[8,64,768]{2,1,0:T(8,128)(2,1)S(1)}, bf16[8,64,768]{2,1,0:T(8,128)(2,1)S(1)}, u32[]{:S(2)}, u32[]{:S(2)}) %collective-permute-start.2) | collective-permute-done | bytes 786464 | tf_op jit(solution)/shard_map/ppermute | solution.py:89
  58.6 2.5 collective-permute-start.6
  61.1 1.1 dynamic-slice_bitcast_fusion.1
  63.8 1.5 collective-permute-start.10
  65.3 1.1 pad_maximum_fusion.10
  66.7 1.2 constant_dynamic-update-slice_fusion.2
  68.0 5.6 collective-permute-done.6
  73.6 1.6 collective-permute-start.14
  75.2 1.1 constant_dynamic-update-slice_fusion.w1_ref
  76.4 8.0 %collective-permute-done.10.d2_ref = bf16[6,64,1024]{2,1,0:T(8,128)(2,1)} collective-permute-done((bf16[6,64,1024]{2,1,0:T(8,128)(2,1)S(1)}, bf16[6,64,1024]{2,1,0:T(8,128)(2,1)}, u32[]{:S(2)}, u32[]{:S(2)}) %collective-permute-start.10) | collective-permute-done | bytes 786464 | tf_op jit(solution)/shard_map/ppermute | solution.py:18
  84.3 22.5 %collective-permute-done.14.refs_8_ = bf16[2,256,1024]{2,1,0:T(8,128)(2,1)} collective-permute-done((bf16[2,256,1024]{2,1,0:T(8,128)(2,1)S(1)}, bf16[2,256,1024]{2,1,0:T(8,128)(2,1)}, u32[]{:S(2)}, u32[]{:S(2)}) %collective-permute-start.14) | collective-permute-done | bytes 1048608 | tf_op jit(solution)/shard_map/ppermute | solution.py:18
  107.3 14.3 %collective-permute-done.11.d3_ref = bf16[6,64,1024]{2,1,0:T(8,128)(2,1)S(1)} collective-permute-done((bf16[6,64,1024]{2,1,0:T(8,128)(2,1)S(1)}, bf16[6,64,1024]{2,1,0:T(8,128)(2,1)S(1)}, u32[]{:S(2)}, u32[]{:S(2)}) %collective-permute-start.11) | collective-permute-done | bytes 786464 | tf_op jit(solution)/shard_map/ppermute | solution.py:89
  122.1 1.5 collective-permute-start.17
  126.0 7.1 %collective-permute-done.15.refs_9_ = bf16[2,256,1024]{2,1,0:T(8,128)(2,1)} collective-permute-done((bf16[2,256,1024]{2,1,0:T(8,128)(2,1)}, bf16[2,256,1024]{2,1,0:T(8,128)(2,1)}, u32[]{:S(2)}, u32[]{:S(2)}) %collective-permute-start.15) | collective-permute-done | bytes 1048608 | tf_op jit(solution)/shard_map/ppermute | solution.py:373
  133.1 37.1 %collective-permute-done.16.refs_10_ = bf16[2,256,1024]{2,1,0:T(8,128)(2,1)} collective-permute-done((bf16[2,256,1024]{2,1,0:T(8,128)(2,1)}, bf16[2,256,1024]{2,1,0:T(8,128)(2,1)}, u32[]{:S(2)}, u32[]{:S(2)}) %collective-permute-start.16) | collective-permute-done | bytes 1048608 | tf_op jit(solution)/shard_map/ppermute | solution.py:373
  170.7 1.4 copy-done.28
  172.2 52.2 %shard_map.254 = (bf16[1536,1024]{1,0:T(8,128)(2,1)}, bf16[1536,3072]{1,0:T(8,128)(2,1)}, bf16[1536,512]{1,0:T(8,128)(2,1)}, bf16[1536,1024]{1,0:T(8,128)(2,1)},...) custom-call(bf16[8,64,768]{2,1,0:T(8,128)(2,1)} %get-tuple-element.120.p0_ref.e0_ref.refs_0_, ...), custom_call_target="tpu_custom_call" | custom-call | flops 16106127360 | bytes 56623104 | tf_op jit(solution)/shard_map/pallas_call | solution.py:175
  225.0 74.9 %shard_map.255 = (bf16[6,64,1024]{2,1,0:T(8,128)(2,1)}, bf16[6,64,1024]{2,1,0:T(8,128)(2,1)}, bf16[6,64,1024]{2,1,0:T(8,128)(2,1)}, bf16[6,64,1024]{2,1,0:T(8,12...) custom-call(bf16[1536,1024]{1,0:T(8,128)(2,1)} %get-tuple-element.51, ...), custom_call_target="tpu_custom_call" | custom-call | flops 51539607552 | bytes 44171264 | tf_op jit(solution)/shard_map/pallas_call | solution.py:318
  299.8 64.8 %shard_map.256 = (bf16[1536,1536]{1,0:T(8,128)(2,1)}, bf16[1536,1536]{1,0:T(8,128)(2,1)}, f32[768,1024]{1,0:T(8,128)}, f32[256,1024]{1,0:T(8,128)}, f32[8,1024]{1,0:T(8,128)}, /*index=5*/f32[1,3072]{1,0:T(1,128)}) custom-call(bf16[1536,3072]{1,0:T(8,128)(2,1)} %get-tuple-element.58.qkv_ref, bf16[1536,1024]{1,0:T(8,128)(2,1)} %get-tuple-element.59.dx_ref.la_ref, ...), custom_call_target="tpu_custom_call" | custom-call | flops 25769803776 | bytes 27353088 | tf_op jit(solution)/shard_map/pallas_call | solution.py:223
  365.2 1.5 collective-permute-start.37
  366.7 1.5 constant_dynamic-slice_fusion
  368.3 16.8 %collective-permute-done.37 = bf16[6,64,1024]{2,1,0:T(8,128)(2,1)} collective-permute-done((bf16[6,64,1024]{2,1,0:T(8,128)(2,1)}, bf16[6,64,1024]{2,1,0:T(8,128)(2,1)}, u32[]{:S(2)}, u32[]{:S(2)}) %collective-permute-start.37) | collective-permute-done | bytes 786464 | tf_op jit(solution)/shard_map/ppermute | solution.py:18
  385.5 19.7 %collective-permute-done.38 = bf16[6,64,1024]{2,1,0:T(8,128)(2,1)S(1)} collective-permute-done((bf16[6,64,1024]{2,1,0:T(8,128)(2,1)}, bf16[6,64,1024]{2,1,0:T(8,128)(2,1)S(1)}, u32[]{:S(2)}, u32[]{:S(2)}) %collective-permute-start.38) | collective-permute-done | bytes 786464 | tf_op jit(solution)/shard_map/ppermute | solution.py:89
  406.1 1.8 dynamic-slice_add_fusion
  407.9 0.9 collective-permute-start.28
  408.9 1.1 collective-permute-start.36
  410.6 34.6 %collective-permute-done.28 = f32[384,1024]{1,0:T(8,128)S(1)} collective-permute-done((f32[384,1024]{1,0:T(8,128)S(1)}, f32[384,1024]{1,0:T(8,128)S(1)}, u32[]{:S(2)}, u32[]{:S(2)}) %collective-permute-start.28) | collective-permute-done | bytes 1572896 | tf_op jit(solution)/shard_map/ppermute | solution.py:18
  448.8 1.0 collective-permute-start.24
  449.9 10.0 %shard_map.257 = f32[1024,768]{1,0:T(8,128)} custom-call(bf16[1536,2560]{1,0:T(8,128)(2,1)} %get-tuple-element.57.la_ref, bf16[1536,2560]{1,0:T(8,128)(2,1)} %collective-permute-done.25.lb_ref.rb_ref.hb_ref, bf16[1536,1536]{1,0:T(8,128)(2,1)} %get-tuple-element.61.ra_ref, bf16[1536,1536]{1,0:T(8,128)(2,1)} %collective-permute-done.26.rb_ref), custom_call_target="tpu_custom_call" | custom-call | flops 4831838208 | bytes 6291456 | tf_op jit(solution)/shard_map/pallas_call | solution.py:335
  460.0 69.6 %collective-permute-done.23 = bf16[6,64,1024]{2,1,0:T(8,128)(2,1)S(1)} collective-permute-done((bf16[6,64,1024]{2,1,0:T(8,128)(2,1)}, bf16[6,64,1024]{2,1,0:T(8,128)(2,1)S(1)}, u32[]{:S(2)}, u32[]{:S(2)}) %collective-permute-start.23) | collective-permute-done | bytes 786464 | tf_op jit(solution)/shard_map/ppermute | solution.py:18
  531.4 2.7 concatenate.87
  534.1 11.2 %collective-permute-done.24 = bf16[6,64,1024]{2,1,0:T(8,128)(2,1)} collective-permute-done((bf16[6,64,1024]{2,1,0:T(8,128)(2,1)}, bf16[6,64,1024]{2,1,0:T(8,128)(2,1)}, u32[]{:S(2)}, u32[]{:S(2)}) %collective-permute-start.24) | collective-permute-done | bytes 786464 | tf_op jit(solution)/shard_map/ppermute | solution.py:89
  546.3 1.0 collective-permute-start.32
  547.3 3.2 maximum_select_fusion.3
  550.5 3.1 pad_maximum_fusion
  554.5 2.1 maximum_select_fusion.2
  556.6 9.6 %shard_map.258 = f32[1024,768]{1,0:T(8,128)} custom-call(bf16[1536,2560]{1,0:T(8,128)(2,1)} %get-tuple-element.57.la_ref, bf16[1536,2560]{1,0:T(8,128)(2,1)} %collective-permute-done.25.lb_ref.rb_ref.hb_ref, bf16[1536,1536]{1,0:T(8,128)(2,1)} %get-tuple-element.61.ra_ref, bf16[1536,1536]{1,0:T(8,128)(2,1)} %collective-permute-done.26.rb_ref), custom_call_target="tpu_custom_call" | custom-call | flops 4831838208 | bytes 6291456 | tf_op jit(solution)/shard_map/pallas_call | solution.py:335
  566.4 1.1 collective-permute-start.31
  567.5 7.8 %shard_map.259 = (f32[1024,256]{1,0:T(8,128)}, f32[1024,256]{1,0:T(8,128)}) custom-call(bf16[1536,1024]{1,0:T(8,128)(2,1)} %get-tuple-element.59.dx_ref.la_ref, bf16[1536,1024]{1,0:T(8,128)(2,1)} %collective-permute-done.33.lb_ref, bf16[1536,512]{1,0:T(8,128)(2,1)} %get-tuple-element.76.ra_ref, bf16[1536,2560]{1,0:T(8,128)(2,1)} %collective-permute-done.25.lb_ref.rb_ref.hb_ref), custom_call_target="tpu_custom_call" | custom-call | flops 3221225472 | bytes 4194304 | tf_op jit(solution)/shard_map/pallas_call | solution.py:335
  575.4 47.6 %collective-permute-done.31 = f32[72,1024]{1,0:T(8,128)S(1)} collective-permute-done((f32[72,1024]{1,0:T(8,128)S(1)}, f32[72,1024]{1,0:T(8,128)S(1)}, u32[]{:S(2)}, u32[]{:S(2)}) %collective-permute-start.31) | collective-permute-done | bytes 294944 | tf_op jit(solution)/shard_map/ppermute | solution.py:18
  623.0 1.1 collective-permute-start.34
  624.1 1.7 maximum_select_fusion.1
  625.8 1.9 maximum_select_fusion
  627.8 1.0 fusion.2
  631.4 16.3 %collective-permute-done.34 = f32[1024,256]{1,0:T(8,128)} collective-permute-done((f32[1024,256]{1,0:T(8,128)}, f32[1024,256]{1,0:T(8,128)}, u32[]{:S(2)}, u32[]{:S(2)}) %collective-permute-start.34) | collective-permute-done | bytes 1048608 | tf_op jit(solution)/shard_map/ppermute | solution.py:18
  647.6 2.4 fusion
  650.0 2.0 copy.36
  652.1 3.3 add_convert_fusion
  655.4 2.6 copy.35
  658.0 51.5 %shard_map.260 = (bf16[1024,1024]{1,0:T(8,128)(2,1)}, bf16[1024,1024]{1,0:T(8,128)(2,1)}, f32[1,1024]{1,0:T(1,128)}) custom-call(bf16[1536,1024]{1,0:T(8,128)(2,1)} %get-tuple-element.51.h_ref.ha_ref, bf16[1536,2048]{1,0:T(8,128)(2,1)} %get-tuple-element.79.ga_ref, bf16[1536,3072]{1,0:T(8,128)(2,1)} %get-tuple-element.80.da_ref, ...), custom_call_target="tpu_custom_call" | custom-call | flops 38654705664 | bytes 8396800 | tf_op jit(solution)/shard_map/pallas_call | solution.py:365
  709.5 1.4 fusion.7
  (155 shorter events, 23.0 us)
Async XLA Ops:
  7.3 23.3 %collective-permute-start = (bf16[8,64,768]{2,1,0:T(8,128)(2,1)}, bf16[8,64,768]{2,1,0:T(8,128)(2,1)}, u32[]{:S(2)}, u32[]{:S(2)}) collective-permute-start(bf16[8,64,768]{2,1,0:T(8,128)(2,1)} %get-tuple-element.118), channel_id=1, source_target_pairs={{0,1},{1,0},{2,3},{3,2},{4,5},{5,4},{6,7},{7,6},{8,9},{9,8},{10,11... | collective-permute-start | bytes 2359304 | tf_op jit(solution)/shard_map/ppermute | solution.py:22
  10.0 15.3 %collective-permute-start.3 = (bf16[256,1024]{1,0:T(8,128)(2,1)S(1)}, bf16[256,1024]{1,0:T(8,128)(2,1)S(1)}, u32[]{:S(2)}, u32[]{:S(2)}) collective-permute-start(bf16[256,1024]{1,0:T(8,128)(2,1)S(1)} %fusion.1), channel_id=1, source_target_pairs={{0,2},{1,3},{2,0},{3,1},{4,6},{5,7},{6,4},{7,5},{8,10},{9,11},{10,... | collective-permute-start | bytes 1572872 | tf_op jit(solution)/shard_map/ppermute | solution.py:18
  12.5 29.6 %collective-permute-start.1 = (bf16[8,64,768]{2,1,0:T(8,128)(2,1)S(1)}, bf16[8,64,768]{2,1,0:T(8,128)(2,1)S(1)}, u32[]{:S(2)}, u32[]{:S(2)}) collective-permute-start(bf16[8,64,768]{2,1,0:T(8,128)(2,1)S(1)} %copy-done.14), channel_id=1, source_target_pairs={{0,2},{1,3},{2,0},{3,1},{4,6},{5,7},{6,4},{7,5},{8,10},{9,11},{10,... | collective-permute-start | bytes 2359304 | tf_op jit(solution)/shard_map/ppermute | solution.py:18
  13.5 17.0 %copy-start = (bf16[24,64,1024]{2,1,0:T(8,128)(2,1)S(1)}, bf16[24,64,1024]{2,1,0:T(8,128)(2,1)}, u32[]{:S(2)}) copy-start(bf16[24,64,1024]{2,1,0:T(8,128)(2,1)} %param.29) | copy-start | bytes 9437188
  13.5 45.1 %collective-permute-start.2 = (bf16[8,64,768]{2,1,0:T(8,128)(2,1)S(1)}, bf16[8,64,768]{2,1,0:T(8,128)(2,1)S(1)}, u32[]{:S(2)}, u32[]{:S(2)}) collective-permute-start(bf16[8,64,768]{2,1,0:T(8,128)(2,1)S(1)} %get-tuple-element.117), channel_id=1, source_target_pairs={{0,3},{1,2},{2,1},{3,0},{4,7},{5,6},{6,5},{7,4},{8,11},{9,10},{10,... | collective-permute-start | bytes 2359304 | tf_op jit(solution)/shard_map/ppermute | solution.py:89
  25.3 36.9 %collective-permute-start.4 = (bf16[256,1024]{1,0:T(8,128)(2,1)S(1)}, bf16[256,1024]{1,0:T(8,128)(2,1)S(1)}, u32[]{:S(2)}, u32[]{:S(2)}) collective-permute-start(bf16[256,1024]{1,0:T(8,128)(2,1)S(1)} %collective-permute-done.3), channel_id=1, source_target_pairs={{0,4},{4,0},{8,12},{12,8},{1,5},{5,1},{9,13},{13,9},{2,6},{6,2},{1... | collective-permute-start | bytes 1572872 | tf_op jit(solution)/shard_map/ppermute | solution.py:373
  27.3 35.0 %collective-permute-start.5 = (bf16[256,1024]{1,0:T(8,128)(2,1)S(1)}, bf16[256,1024]{1,0:T(8,128)(2,1)S(1)}, u32[]{:S(2)}, u32[]{:S(2)}) collective-permute-start(bf16[256,1024]{1,0:T(8,128)(2,1)S(1)} %collective-permute-done.3), channel_id=1, source_target_pairs={{0,8},{4,12},{8,0},{12,4},{1,9},{5,13},{9,1},{13,5},{2,10},{6,14},... | collective-permute-start | bytes 1572872 | tf_op jit(solution)/shard_map/ppermute | solution.py:373
  30.5 91.5 %collective-permute-start.7 = (bf16[1024,1024]{1,0:T(8,128)(2,1)}, bf16[1024,1024]{1,0:T(8,128)(2,1)}, u32[]{:S(2)}, u32[]{:S(2)}) collective-permute-start(bf16[1024,1024]{1,0:T(8,128)(2,1)} %pad_maximum_fusion.1.w0_ref), channel_id=1, source_target_pairs={{0,1},{1,0},{2,3},{3,2},{4,5},{5,4},{6,7},{7,6},{8,9},{9,8},{10,11... | collective-permute-start | bytes 6291464 | tf_op jit(solution)/shard_map/ppermute | solution.py:22
  32.0 34.3 %copy-start.5 = (bf16[6,64,1024]{2,1,0:T(8,128)(2,1)}, bf16[6,64,1024]{2,1,0:T(8,128)(2,1)S(1)}, u32[]{:S(2)}) copy-start(bf16[6,64,1024]{2,1,0:T(8,128)(2,1)S(1)} %get-tuple-element.83) | copy-start | bytes 2359300
  42.1 23.2 %copy-start.29 = (bf16[8,64,768]{2,1,0:T(8,128)(2,1)}, bf16[8,64,768]{2,1,0:T(8,128)(2,1)S(1)}, u32[]{:S(2)}) copy-start(bf16[8,64,768]{2,1,0:T(8,128)(2,1)S(1)} %collective-permute-done.1.p2_ref.e2_ref.refs_1_) | copy-start | bytes 2359300
  42.1 34.2 %collective-permute-start.9 = (bf16[6,64,1024]{2,1,0:T(8,128)(2,1)}, bf16[6,64,1024]{2,1,0:T(8,128)(2,1)}, u32[]{:S(2)}, u32[]{:S(2)}) collective-permute-start(bf16[6,64,1024]{2,1,0:T(8,128)(2,1)} %get-tuple-element.107), channel_id=1, source_target_pairs={{0,1},{1,0},{2,3},{3,2},{4,5},{5,4},{6,7},{7,6},{8,9},{9,8},{10,11... | collective-permute-start | bytes 2359304 | tf_op jit(solution)/shard_map/ppermute | solution.py:22
  58.6 6.7 copy-start.30
  58.6 15.0 %collective-permute-start.6 = (bf16[256,1024]{1,0:T(8,128)(2,1)S(1)}, bf16[256,1024]{1,0:T(8,128)(2,1)}, u32[]{:S(2)}, u32[]{:S(2)}) collective-permute-start(bf16[256,1024]{1,0:T(8,128)(2,1)S(1)} %collective-permute-done.3), channel_id=1, source_target_pairs={{0,12},{4,8},{8,4},{12,0},{1,13},{5,9},{9,5},{13,1},{2,14},{6,10},... | collective-permute-start | bytes 1572872 | tf_op jit(solution)/shard_map/ppermute | solution.py:373
  62.2 61.4 %collective-permute-start.12 = (bf16[1024,1024]{1,0:T(8,128)(2,1)}, bf16[1024,1024]{1,0:T(8,128)(2,1)}, u32[]{:S(2)}, u32[]{:S(2)}) collective-permute-start(bf16[1024,1024]{1,0:T(8,128)(2,1)} %w1_ref.1), channel_id=1, source_target_pairs={{0,1},{1,0},{2,3},{3,2},{4,5},{5,4},{6,7},{7,6},{8,9},{9,8},{10,11... | collective-permute-start | bytes 6291464 | tf_op jit(solution)/shard_map/ppermute | solution.py:22
  63.8 20.5 %collective-permute-start.10 = (bf16[6,64,1024]{2,1,0:T(8,128)(2,1)S(1)}, bf16[6,64,1024]{2,1,0:T(8,128)(2,1)}, u32[]{:S(2)}, u32[]{:S(2)}) collective-permute-start(bf16[6,64,1024]{2,1,0:T(8,128)(2,1)S(1)} %get-tuple-element.83), channel_id=1, source_target_pairs={{0,2},{1,3},{2,0},{3,1},{4,6},{5,7},{6,4},{7,5},{8,10},{9,11},{10,... | collective-permute-start | bytes 2359304 | tf_op jit(solution)/shard_map/ppermute | solution.py:18
  66.6 7.0 copy-start.9
  66.6 17.7 %copy-start.11 = (bf16[6,64,1024]{2,1,0:T(8,128)(2,1)S(1)}, bf16[6,64,1024]{2,1,0:T(8,128)(2,1)}, u32[]{:S(2)}) copy-start(bf16[6,64,1024]{2,1,0:T(8,128)(2,1)} %get-tuple-element.105) | copy-start | bytes 2359300
  66.7 57.6 %copy-start.25 = (bf16[1024]{0:T(1024)(128)(2,1)S(1)}, bf16[1024]{0:T(1024)(128)(2,1)}, u32[]{:S(2)}) copy-start(bf16[1024]{0:T(1024)(128)(2,1)} %param.17) | copy-start | bytes 6148
  66.7 58.2 %copy-start.26 = (bf16[1024]{0:T(1024)(128)(2,1)S(1)}, bf16[1024]{0:T(1024)(128)(2,1)}, u32[]{:S(2)}) copy-start(bf16[1024]{0:T(1024)(128)(2,1)} %param.24) | copy-start | bytes 6148
  66.7 58.8 %copy-start.27 = (bf16[1024]{0:T(1024)(128)(2,1)S(1)}, bf16[1024]{0:T(1024)(128)(2,1)}, u32[]{:S(2)}) copy-start(bf16[1024]{0:T(1024)(128)(2,1)} %param.28) | copy-start | bytes 6148
  73.6 33.2 %collective-permute-start.14 = (bf16[2,256,1024]{2,1,0:T(8,128)(2,1)S(1)}, bf16[2,256,1024]{2,1,0:T(8,128)(2,1)}, u32[]{:S(2)}, u32[]{:S(2)}) collective-permute-start(bf16[2,256,1024]{2,1,0:T(8,128)(2,1)S(1)} %copy-done.9), channel_id=1, source_target_pairs={{0,2},{1,3},{2,0},{3,1},{4,6},{5,7},{6,4},{7,5},{8,10},{9,11},{10,... | collective-permute-start | bytes 3145736 | tf_op jit(solution)/shard_map/ppermute | solution.py:18
  76.3 95.9 %copy-start.8 = (bf16[1024,1024]{1,0:T(8,128)(2,1)}, bf16[1024,1024]{1,0:T(8,128)(2,1)S(1)}, u32[]{:S(2)}) copy-start(bf16[1024,1024]{1,0:T(8,128)(2,1)S(1)} %constant_dynamic-update-slice_fusion.w1_ref) | copy-start | bytes 6291460
  76.3 94.4 %collective-permute-start.8 = (bf16[1024,1024]{1,0:T(8,128)(2,1)S(1)}, bf16[1024,1024]{1,0:T(8,128)(2,1)S(1)}, u32[]{:S(2)}, u32[]{:S(2)}) collective-permute-start(bf16[1024,1024]{1,0:T(8,128)(2,1)S(1)} %constant_dynamic-update-slice_fusion.w1_ref), channel_id=1, source_target_pairs={{0,1},{1,0},{2,3},{3,2},{4,5},{5,4},{6,7},{7,6},{8,9},{9,8},{10,11... | collective-permute-start | bytes 6291464 | tf_op jit(solution)/shard_map/ppermute | solution.py:22
  84.3 37.3 %collective-permute-start.11 = (bf16[6,64,1024]{2,1,0:T(8,128)(2,1)S(1)}, bf16[6,64,1024]{2,1,0:T(8,128)(2,1)S(1)}, u32[]{:S(2)}, u32[]{:S(2)}) collective-permute-start(bf16[6,64,1024]{2,1,0:T(8,128)(2,1)S(1)} %copy-done.11), channel_id=1, source_target_pairs={{0,3},{1,2},{2,1},{3,0},{4,7},{5,6},{6,5},{7,4},{8,11},{9,10},{10,... | collective-permute-start | bytes 2359304 | tf_op jit(solution)/shard_map/ppermute | solution.py:89
  106.8 26.3 %collective-permute-start.15 = (bf16[2,256,1024]{2,1,0:T(8,128)(2,1)}, bf16[2,256,1024]{2,1,0:T(8,128)(2,1)}, u32[]{:S(2)}, u32[]{:S(2)}) collective-permute-start(bf16[2,256,1024]{2,1,0:T(8,128)(2,1)} %collective-permute-done.14.refs_8_), channel_id=1, source_target_pairs={{0,4},{4,0},{8,12},{12,8},{1,5},{5,1},{9,13},{13,9},{2,6},{6,2},{1... | collective-permute-start | bytes 3145736 | tf_op jit(solution)/shard_map/ppermute | solution.py:373
  121.6 102.9 %copy-start.31 = (bf16[6,64,1024]{2,1,0:T(8,128)(2,1)}, bf16[6,64,1024]{2,1,0:T(8,128)(2,1)S(1)}, u32[]{:S(2)}) copy-start(bf16[6,64,1024]{2,1,0:T(8,128)(2,1)S(1)} %collective-permute-done.11.d3_ref) | copy-start | bytes 2359300
  121.6 48.6 %collective-permute-start.16 = (bf16[2,256,1024]{2,1,0:T(8,128)(2,1)}, bf16[2,256,1024]{2,1,0:T(8,128)(2,1)}, u32[]{:S(2)}, u32[]{:S(2)}) collective-permute-start(bf16[2,256,1024]{2,1,0:T(8,128)(2,1)} %collective-permute-done.14.refs_8_), channel_id=1, source_target_pairs={{0,8},{4,12},{8,0},{12,4},{1,9},{5,13},{9,1},{13,5},{2,10},{6,14},... | collective-permute-start | bytes 3145736 | tf_op jit(solution)/shard_map/ppermute | solution.py:373
  122.1 48.3 %collective-permute-start.17 = (bf16[2,256,1024]{2,1,0:T(8,128)(2,1)}, bf16[2,256,1024]{2,1,0:T(8,128)(2,1)}, u32[]{:S(2)}, u32[]{:S(2)}) collective-permute-start(bf16[2,256,1024]{2,1,0:T(8,128)(2,1)} %collective-permute-done.14.refs_8_), channel_id=1, source_target_pairs={{0,12},{4,8},{8,4},{12,0},{1,13},{5,9},{9,5},{13,1},{2,14},{6,10},... | collective-permute-start | bytes 3145736 | tf_op jit(solution)/shard_map/ppermute | solution.py:373
  123.6 100.9 %collective-permute-start.13 = (bf16[1024,1024]{1,0:T(8,128)(2,1)}, bf16[1024,1024]{1,0:T(8,128)(2,1)}, u32[]{:S(2)}, u32[]{:S(2)}) collective-permute-start(bf16[1024,1024]{1,0:T(8,128)(2,1)} %w2_ref.1), channel_id=1, source_target_pairs={{0,1},{1,0},{2,3},{3,2},{4,5},{5,4},{6,7},{7,6},{8,9},{9,8},{10,11... | collective-permute-start | bytes 6291464 | tf_op jit(solution)/shard_map/ppermute | solution.py:22
  133.1 91.8 %collective-permute-start.18 = (bf16[2,256,1024]{2,1,0:T(8,128)(2,1)}, bf16[2,256,1024]{2,1,0:T(8,128)(2,1)}, u32[]{:S(2)}, u32[]{:S(2)}) collective-permute-start(bf16[2,256,1024]{2,1,0:T(8,128)(2,1)} %collective-permute-done.14.refs_8_), channel_id=1, source_target_pairs={{0,1},{1,0},{2,3},{3,2},{4,5},{5,4},{6,7},{7,6},{8,9},{9,8},{10,11... | collective-permute-start | bytes 3145736 | tf_op jit(solution)/shard_map/ppermute | solution.py:22
  170.2 54.7 %collective-permute-start.19 = (bf16[2,256,1024]{2,1,0:T(8,128)(2,1)}, bf16[2,256,1024]{2,1,0:T(8,128)(2,1)}, u32[]{:S(2)}, u32[]{:S(2)}) collective-permute-start(bf16[2,256,1024]{2,1,0:T(8,128)(2,1)} %collective-permute-done.15.refs_9_), channel_id=1, source_target_pairs={{0,1},{1,0},{2,3},{3,2},{4,5},{5,4},{6,7},{7,6},{8,9},{9,8},{10,11... | collective-permute-start | bytes 3145736 | tf_op jit(solution)/shard_map/ppermute | solution.py:22
  170.3 54.6 %collective-permute-start.20 = (bf16[2,256,1024]{2,1,0:T(8,128)(2,1)}, bf16[2,256,1024]{2,1,0:T(8,128)(2,1)}, u32[]{:S(2)}, u32[]{:S(2)}) collective-permute-start(bf16[2,256,1024]{2,1,0:T(8,128)(2,1)} %collective-permute-done.16.refs_10_), channel_id=1, source_target_pairs={{0,1},{1,0},{2,3},{3,2},{4,5},{5,4},{6,7},{7,6},{8,9},{9,8},{10,11... | collective-permute-start | bytes 3145736 | tf_op jit(solution)/shard_map/ppermute | solution.py:22
  172.1 52.8 %collective-permute-start.21 = (bf16[2,256,1024]{2,1,0:T(8,128)(2,1)}, bf16[2,256,1024]{2,1,0:T(8,128)(2,1)}, u32[]{:S(2)}, u32[]{:S(2)}) collective-permute-start(bf16[2,256,1024]{2,1,0:T(8,128)(2,1)} %collective-permute-done.17.refs_11_), channel_id=1, source_target_pairs={{0,1},{1,0},{2,3},{3,2},{4,5},{5,4},{6,7},{7,6},{8,9},{9,8},{10,11... | collective-permute-start | bytes 3145736 | tf_op jit(solution)/shard_map/ppermute | solution.py:22
  224.5 224.3 %collective-permute-start.25 = (bf16[1536,2560]{1,0:T(8,128)(2,1)}, bf16[1536,2560]{1,0:T(8,128)(2,1)}, u32[]{:S(2)}, u32[]{:S(2)}) collective-permute-start(bf16[1536,2560]{1,0:T(8,128)(2,1)} %get-tuple-element.57.la_ref), channel_id=1, source_target_pairs={{0,1},{1,0},{2,3},{3,2},{4,5},{5,4},{6,7},{7,6},{8,9},{9,8},{10,11... | collective-permute-start | bytes 23592968 | tf_op jit(solution)/shard_map/ppermute | solution.py:22
  364.7 41.4 %copy-start.4 = (f32[768,1024]{1,0:T(8,128)S(1)}, f32[768,1024]{1,0:T(8,128)}, u32[]{:S(2)}) copy-start(f32[768,1024]{1,0:T(8,128)} %get-tuple-element.67) | copy-start | bytes 9437188
  364.7 80.6 %collective-permute-start.26 = (bf16[1536,1536]{1,0:T(8,128)(2,1)}, bf16[1536,1536]{1,0:T(8,128)(2,1)}, u32[]{:S(2)}, u32[]{:S(2)}) collective-permute-start(bf16[1536,1536]{1,0:T(8,128)(2,1)} %get-tuple-element.62), channel_id=1, source_target_pairs={{0,1},{1,0},{2,3},{3,2},{4,5},{5,4},{6,7},{7,6},{8,9},{9,8},{10,11... | collective-permute-start | bytes 14155784 | tf_op jit(solution)/shard_map/ppermute | solution.py:22
  364.8 293.2 %collective-permute-start.35 = (bf16[1536,3072]{1,0:T(8,128)(2,1)}, bf16[1536,3072]{1,0:T(8,128)(2,1)}, u32[]{:S(2)}, u32[]{:S(2)}) collective-permute-start(bf16[1536,3072]{1,0:T(8,128)(2,1)} %get-tuple-element.80.da_ref), channel_id=1, source_target_pairs={{0,1},{1,0},{2,3},{3,2},{4,5},{5,4},{6,7},{7,6},{8,9},{9,8},{10,11... | collective-permute-start | bytes 28311560 | tf_op jit(solution)/shard_map/ppermute | solution.py:22
  365.2 19.9 %collective-permute-start.37 = (bf16[6,64,1024]{2,1,0:T(8,128)(2,1)}, bf16[6,64,1024]{2,1,0:T(8,128)(2,1)}, u32[]{:S(2)}, u32[]{:S(2)}) collective-permute-start(bf16[6,64,1024]{2,1,0:T(8,128)(2,1)} %get-tuple-element.108.d0_ref), channel_id=1, source_target_pairs={{0,2},{1,3},{2,0},{3,1},{4,6},{5,7},{6,4},{7,5},{8,10},{9,11},{10,... | collective-permute-start | bytes 2359304 | tf_op jit(solution)/shard_map/ppermute | solution.py:18
  368.2 37.0 %collective-permute-start.27 = (f32[384,1024]{1,0:T(8,128)S(1)}, f32[384,1024]{1,0:T(8,128)}, u32[]{:S(2)}, u32[]{:S(2)}) collective-permute-start(f32[384,1024]{1,0:T(8,128)S(1)} %constant_dynamic-slice_fusion), channel_id=1, source_target_pairs={{0,1},{1,0},{2,3},{3,2},{4,5},{5,4},{6,7},{7,6},{8,9},{9,8},{10,11... | collective-permute-start | bytes 4718600 | tf_op jit(solution)/shard_map/ppermute | solution.py:22
  385.1 20.0 %collective-permute-start.38 = (bf16[6,64,1024]{2,1,0:T(8,128)(2,1)}, bf16[6,64,1024]{2,1,0:T(8,128)(2,1)S(1)}, u32[]{:S(2)}, u32[]{:S(2)}) collective-permute-start(bf16[6,64,1024]{2,1,0:T(8,128)(2,1)} %get-tuple-element.107), channel_id=1, source_target_pairs={{0,3},{1,2},{2,1},{3,0},{4,7},{5,6},{6,5},{7,4},{8,11},{9,10},{10,... | collective-permute-start | bytes 2359304 | tf_op jit(solution)/shard_map/ppermute | solution.py:89
  405.1 2.8 collective-permute-start.39
  406.0 2.9 collective-permute-start.22
  406.1 3.9 copy-start.1
  407.9 37.3 %collective-permute-start.28 = (f32[384,1024]{1,0:T(8,128)S(1)}, f32[384,1024]{1,0:T(8,128)S(1)}, u32[]{:S(2)}, u32[]{:S(2)}) collective-permute-start(f32[384,1024]{1,0:T(8,128)S(1)} %dynamic-slice_add_fusion), channel_id=1, source_target_pairs={{0,2},{1,3},{2,0},{3,1},{4,6},{5,7},{6,4},{7,5},{8,10},{9,11},{10,... | collective-permute-start | bytes 4718600 | tf_op jit(solution)/shard_map/ppermute | solution.py:18
  408.9 141.6 %collective-permute-start.36 = (bf16[1536,1024]{1,0:T(8,128)(2,1)}, bf16[1536,1024]{1,0:T(8,128)(2,1)}, u32[]{:S(2)}, u32[]{:S(2)}) collective-permute-start(bf16[1536,1024]{1,0:T(8,128)(2,1)} %get-tuple-element.51.h_ref.ha_ref), channel_id=1, source_target_pairs={{0,2},{1,3},{2,0},{3,1},{4,6},{5,7},{6,4},{7,5},{8,10},{9,11},{10,... | collective-permute-start | bytes 9437192 | tf_op jit(solution)/shard_map/ppermute | solution.py:18
  445.2 121.2 %collective-permute-start.33 = (bf16[1536,1024]{1,0:T(8,128)(2,1)}, bf16[1536,1024]{1,0:T(8,128)(2,1)}, u32[]{:S(2)}, u32[]{:S(2)}) collective-permute-start(bf16[1536,1024]{1,0:T(8,128)(2,1)} %get-tuple-element.59.dx_ref.la_ref), channel_id=1, source_target_pairs={{0,1},{1,0},{2,3},{3,2},{4,5},{5,4},{6,7},{7,6},{8,9},{9,8},{10,11... | collective-permute-start | bytes 9437192 | tf_op jit(solution)/shard_map/ppermute | solution.py:22
  445.3 84.3 %collective-permute-start.23 = (bf16[6,64,1024]{2,1,0:T(8,128)(2,1)}, bf16[6,64,1024]{2,1,0:T(8,128)(2,1)S(1)}, u32[]{:S(2)}, u32[]{:S(2)}) collective-permute-start(bf16[6,64,1024]{2,1,0:T(8,128)(2,1)} %get-tuple-element.55), channel_id=1, source_target_pairs={{0,2},{1,3},{2,0},{3,1},{4,6},{5,7},{6,4},{7,5},{8,10},{9,11},{10,... | collective-permute-start | bytes 2359304 | tf_op jit(solution)/shard_map/ppermute | solution.py:18
  448.8 96.5 %collective-permute-start.24 = (bf16[6,64,1024]{2,1,0:T(8,128)(2,1)}, bf16[6,64,1024]{2,1,0:T(8,128)(2,1)}, u32[]{:S(2)}, u32[]{:S(2)}) collective-permute-start(bf16[6,64,1024]{2,1,0:T(8,128)(2,1)} %get-tuple-element.56), channel_id=1, source_target_pairs={{0,3},{1,2},{2,1},{3,0},{4,7},{5,6},{6,5},{7,4},{8,11},{9,10},{10,... | collective-permute-start | bytes 2359304 | tf_op jit(solution)/shard_map/ppermute | solution.py:89
  449.9 10.0 %copy-start.3 = (f32[256,1024]{1,0:T(8,128)S(1)}, f32[256,1024]{1,0:T(8,128)}, u32[]{:S(2)}) copy-start(f32[256,1024]{1,0:T(8,128)} %get-tuple-element.71) | copy-start | bytes 3145732
  449.9 79.6 %copy-start.22 = (f32[1,3072]{1,0:T(1,128)S(1)}, f32[1,3072]{1,0:T(1,128)}, u32[]{:S(2)}) copy-start(f32[1,3072]{1,0:T(1,128)} %get-tuple-element.74) | copy-start | bytes 36868
  459.9 85.8 %copy-start.23 = (bf16[1024]{0:T(1024)(128)(2,1)S(1)}, bf16[1024]{0:T(1024)(128)(2,1)}, u32[]{:S(2)}) copy-start(bf16[1024]{0:T(1024)(128)(2,1)} %param.26) | copy-start | bytes 6148
  529.5 16.8 %collective-permute-start.29 = (bf16[384,1024]{1,0:T(8,128)(2,1)S(1)}, bf16[384,1024]{1,0:T(8,128)(2,1)}, u32[]{:S(2)}, u32[]{:S(2)}) collective-permute-start(bf16[384,1024]{1,0:T(8,128)(2,1)S(1)} %add_convert_fusion.1), channel_id=1, source_target_pairs={{0,1},{1,0},{2,3},{3,2},{4,5},{5,4},{6,7},{7,6},{8,9},{9,8},{10,11... | collective-permute-start | bytes 2359304 | tf_op jit(solution)/shard_map/ppermute | solution.py:22
  531.3 19.2 %copy-start.6 = (bf16[6,64,1024]{2,1,0:T(8,128)(2,1)S(1)}, bf16[6,64,1024]{2,1,0:T(8,128)(2,1)}, u32[]{:S(2)}) copy-start(bf16[6,64,1024]{2,1,0:T(8,128)(2,1)} %copy-done.5) | copy-start | bytes 2359300
  545.3 8.3 %collective-permute-start.30 = (f32[138,1024]{1,0:T(8,128)}, f32[138,1024]{1,0:T(8,128)S(1)}, u32[]{:S(2)}, u32[]{:S(2)}) collective-permute-start(f32[138,1024]{1,0:T(8,128)} %concatenate.87), channel_id=1, source_target_pairs={{0,1},{1,0},{2,3},{3,2},{4,5},{5,4},{6,7},{7,6},{8,9},{9,8},{10,11... | collective-permute-start | bytes 1695752 | tf_op jit(solution)/shard_map/ppermute | solution.py:22
  546.3 105.8 %collective-permute-start.32 = (f32[1024,768]{1,0:T(8,128)}, f32[1024,768]{1,0:T(8,128)}, u32[]{:S(2)}, u32[]{:S(2)}) collective-permute-start(f32[1024,768]{1,0:T(8,128)} %shard_map.257), channel_id=1, source_target_pairs={{0,2},{1,3},{2,0},{3,1},{4,6},{5,7},{6,4},{7,5},{8,10},{9,11},{10,... | collective-permute-start | bytes 9437192 | tf_op jit(solution)/shard_map/ppermute | solution.py:18
  550.5 107.5 %collective-permute-start.40 = (bf16[1536,1024]{1,0:T(8,128)(2,1)}, bf16[1536,1024]{1,0:T(8,128)(2,1)}, u32[]{:S(2)}, u32[]{:S(2)}) collective-permute-start(bf16[1536,1024]{1,0:T(8,128)(2,1)} %collective-permute-done.36.hx_ref), channel_id=1, source_target_pairs={{0,1},{1,0},{2,3},{3,2},{4,5},{5,4},{6,7},{7,6},{8,9},{9,8},{10,11... | collective-permute-start | bytes 9437192 | tf_op jit(solution)/shard_map/ppermute | solution.py:22
  553.6 104.4 %collective-permute-start.41 = (bf16[1536,1024]{1,0:T(8,128)(2,1)}, bf16[1536,1024]{1,0:T(8,128)(2,1)}, u32[]{:S(2)}, u32[]{:S(2)}) collective-permute-start(bf16[1536,1024]{1,0:T(8,128)(2,1)} %bitcast.18.dx_ref), channel_id=1, source_target_pairs={{0,1},{1,0},{2,3},{3,2},{4,5},{5,4},{6,7},{7,6},{8,9},{9,8},{10,11... | collective-permute-start | bytes 9437192 | tf_op jit(solution)/shard_map/ppermute | solution.py:22
  556.6 9.7 %copy-start.16 = (f32[138,1024]{1,0:T(8,128)S(1)}, f32[138,1024]{1,0:T(8,128)}, u32[]{:S(2)}) copy-start(f32[138,1024]{1,0:T(8,128)} %copy-done.15) | copy-start | bytes 1695748
  566.4 61.4 %copy-start.7 = (f32[138,1024]{1,0:T(8,128)}, f32[138,1024]{1,0:T(8,128)S(1)}, u32[]{:S(2)}) copy-start(f32[138,1024]{1,0:T(8,128)S(1)} %add.125) | copy-start | bytes 1695748
  566.4 56.5 %collective-permute-start.31 = (f32[72,1024]{1,0:T(8,128)S(1)}, f32[72,1024]{1,0:T(8,128)S(1)}, u32[]{:S(2)}, u32[]{:S(2)}) collective-permute-start(f32[72,1024]{1,0:T(8,128)S(1)} %pad_maximum_fusion.11), channel_id=1, source_target_pairs={{0,2},{1,3},{2,0},{3,1},{4,6},{5,7},{6,4},{7,5},{8,10},{9,11},{10,... | collective-permute-start | bytes 884744 | tf_op jit(solution)/shard_map/ppermute | solution.py:18
  567.5 56.5 %copy-start.12 = (bf16[6,64,1024]{2,1,0:T(8,128)(2,1)S(1)}, bf16[6,64,1024]{2,1,0:T(8,128)(2,1)}, u32[]{:S(2)}) copy-start(bf16[6,64,1024]{2,1,0:T(8,128)(2,1)} %get-tuple-element.63) | copy-start | bytes 2359300
  623.0 4.7 copy-start.21
  623.0 24.6 %collective-permute-start.34 = (f32[1024,256]{1,0:T(8,128)}, f32[1024,256]{1,0:T(8,128)}, u32[]{:S(2)}, u32[]{:S(2)}) collective-permute-start(f32[1024,256]{1,0:T(8,128)} %get-tuple-element.78), channel_id=1, source_target_pairs={{0,2},{1,3},{2,0},{3,1},{4,6},{5,7},{6,4},{7,5},{8,10},{9,11},{10,... | collective-permute-start | bytes 3145736 | tf_op jit(solution)/shard_map/ppermute | solution.py:18
  628.8 23.3 %copy-start.2 = (f32[1024,768]{1,0:T(8,128)S(1)}, f32[1024,768]{1,0:T(8,128)}, u32[]{:S(2)}) copy-start(f32[1024,768]{1,0:T(8,128)} %shard_map.258) | copy-start | bytes 9437188
  (10 other events, 15.6 us)
